TPU v7x, 1024 devices: a whole 4x4x32 slice. The times are simulated.
1024 devices in a mesh: outer: 16 (over x, y), inner: 8 (over z_lo), tensor: 8 (over z_hi, core).
Axes of the slice: x: 4, y: 4, z: 32 (z_hi: 4, z_lo: 8; z = z_hi * 8 + z_lo), core: 2. Of those that a mesh axis runs over, the one named last changes fastest.
Arguments:
- queries: bfloat16 [16384, 4096], P(('outer', 'inner'), 'tensor')
- keys: bfloat16 [16384, 1024], P(('outer', 'inner'), 'tensor')
- values: bfloat16 [16384, 1024], P(('outer', 'inner'), 'tensor'), may hold values from -6 to 6
- stretch_order: int32 [256], replicated, may hold values from 0 to 255, as said below
- w_out: bfloat16 [4096, 8192], P('tensor'), may hold values from -0.125 to 0.125
Outputs:
- mixed: bfloat16 [16384, 8192], P(('outer', 'inner'), 'tensor')
Inputs may be any that keep to these rules, and one draw needn't show every extreme that they name: stretch_order is a permutation of 0 to 255, and storage stretches 2 d and 2 d + 1 hold sequence stretches j and 255 - j for some j < 128.
All inputs are finite; a program needn't handle non-finite values.
Results may differ from a plain program's by a relative error of at most 0.015.
Values may be sent and summed in bfloat16 or wider, within the bound.
No kernel may reach another device: no remote copies, remote signals or barrier semaphores. Data moves between devices by JAX's collectives and lax.ppermute only.
A program may use at most 64 MiB of HBM per device.

v0:
```python
import math

import jax
import jax.numpy as jnp
from jax import lax
from jax.experimental import pallas as pl
from jax.experimental.pallas import tpu as pltpu
from jax.sharding import PartitionSpec as P


HD = 128
HEADS = 4
CH = 64
ROWS = 2 * CH
OUTER = 16
INNER = 8
FAR = 4
ZHI = 4
QC = HEADS * CH
EXTRA = 16
NEG = -1e30
COEF = math.log2(math.e) / math.sqrt(HD)
PER = 2
HALF = 512


def dot(a, b, dims):
    return lax.dot_general(a, b, (dims, ((), ())), preferred_element_type=jnp.float32)


def three_terms(x):
    hi = x.astype(jnp.bfloat16)
    rest = x - hi.astype(jnp.float32)
    mid = rest.astype(jnp.bfloat16)
    low = (rest - mid.astype(jnp.float32)).astype(jnp.bfloat16)
    return hi.astype(jnp.float32), mid.astype(jnp.float32), low.astype(jnp.float32)


def attention_kernel(own_ref, sel_ref, q_ref, *refs):
    pairs = refs[:FAR]
    late_ref, oe_ref, ol_ref, pick, dense, vt_dense, vt_e, vt_l = refs[FAR:]

    def rows_of(s, at):
        first = (s // FAR) * 2 * ROWS + at
        return pairs[s % FAR][first : first + CH, :]

    step = pl.program_id(0)
    keys_dense = INNER * CH

    @pl.when(step == 0)
    def _():
        zero = jnp.zeros((CH, HD), jnp.bfloat16)
        for s in range(INNER):
            k_e = rows_of(s, 0)
            k_l = rows_of(s, CH)
            pick[s, 0] = jnp.concatenate([k_e, zero], axis=1)
            pick[s, 1] = jnp.concatenate([zero, k_l], axis=1)
            dense[s * CH : (s + 1) * CH, :] = jnp.concatenate([zero, k_e], axis=1)
        dense[keys_dense:, :] = jnp.concatenate([zero, rows_of(0, CH)], axis=1)
        v_e = jnp.concatenate([rows_of(s, ROWS) for s in range(INNER)], axis=0)
        v_l = jnp.concatenate([rows_of(s, ROWS + CH) for s in range(INNER)], axis=0)
        t_e = v_e.astype(jnp.float32).T.astype(jnp.bfloat16)
        t_l = v_l.astype(jnp.float32).T.astype(jnp.bfloat16)
        vt_e[...] = t_e
        vt_l[...] = t_l
        vt_dense[:, :keys_dense] = t_e
        vt_dense[:, keys_dense:] = t_l[:, :CH]

    key_at = lax.broadcasted_iota(jnp.int32, (CH, QC), 0)
    query_at = lax.broadcasted_iota(jnp.int32, (CH, QC), 1) % CH
    causal = key_at <= query_at

    for p in range(PER):
        a = step * PER + p
        own = a == own_ref[0]
        q = q_ref[p]
        stacked = [
            jnp.concatenate([q[r : r + CH, h * HD : (h + 1) * HD] for h in range(HEADS)], axis=0)
            for r in (0, CH)
        ]
        q_cat = jnp.concatenate(stacked, axis=1)
        s_dense = dot(dense[...], q_cat, ((1,), (1,)))
        late = [sel_ref[a * INNER + s] > 0 for s in range(INNER)]
        chosen = jnp.concatenate([pick[s, sel_ref[a * INNER + s]] for s in range(INNER)], axis=0)
        s_sel = dot(chosen, q_cat, ((1,), (1,)))
        keep = jnp.where(own, 1, 0)
        s_first = jnp.where(jnp.logical_or(causal, keep == 0), s_sel[:CH], NEG)
        s_extra = jnp.where(jnp.logical_and(causal, keep == 1), s_dense[keys_dense:], NEG)
        blocks = [s_first] + [s_sel[s * CH : (s + 1) * CH] for s in range(1, INNER)]
        tops = [jnp.max(b, axis=0, keepdims=True) for b in blocks]
        m_e = jnp.full((1, QC), NEG, jnp.float32)
        m_l = jnp.maximum(
            jnp.max(s_dense[:keys_dense], axis=0, keepdims=True),
            jnp.max(s_extra, axis=0, keepdims=True),
        )
        for s in range(INNER):
            m_e = jnp.maximum(m_e, jnp.where(late[s], NEG, tops[s]))
            m_l = jnp.maximum(m_l, jnp.where(late[s], tops[s], NEG))
        p_dense = jnp.exp2((s_dense[:keys_dense] - m_l) * COEF)
        p_extra = jnp.exp2((s_extra - m_l) * COEF)
        l_l = jnp.sum(p_dense, axis=0, keepdims=True) + jnp.sum(p_extra, axis=0, keepdims=True)
        l_e = jnp.zeros((1, QC), jnp.float32)
        weights = []
        for s in range(INNER):
            w = jnp.exp2((blocks[s] - jnp.where(late[s], m_l, m_e)) * COEF)
            part = jnp.sum(w, axis=0, keepdims=True)
            l_e = l_e + jnp.where(late[s], 0.0, part)
            l_l = l_l + jnp.where(late[s], part, 0.0)
            weights.append(w.astype(jnp.bfloat16))
        w_sel = jnp.concatenate(weights, axis=0)
        w_dense = jnp.concatenate([p_dense.astype(jnp.bfloat16), p_extra.astype(jnp.bfloat16)], axis=0)
        is_late = late_ref[p, 0:1, :]
        v_sel = jnp.concatenate([vt_e[...] * (1 - is_late), vt_l[...] * is_late], axis=0)
        o_sel = dot(v_sel, w_sel, ((1,), (0,)))
        o_e = o_sel[:HD]
        o_l = o_sel[HD:] + dot(vt_dense[...], w_dense, ((1,), (0,)))
        some = l_e > 0.0
        inv_e = jnp.where(some, 1.0 / jnp.where(some, l_e, 1.0), 0.0)
        lse_e = jnp.where(some, m_e * COEF + jnp.log2(jnp.where(some, l_e, 1.0)), NEG)
        lse_l = m_l * COEF + jnp.log2(l_l)
        for ref, o_t, inv, lse in ((oe_ref, o_e, inv_e, lse_e), (ol_ref, o_l, 1.0 / l_l, lse_l)):
            ref[p, :HD, :] = (o_t * inv).astype(jnp.bfloat16)
            rows = list(three_terms(lse)) + [jnp.zeros((EXTRA - 3, QC), jnp.float32)]
            ref[p, HD:, :] = jnp.concatenate(rows, axis=0).astype(jnp.bfloat16)


def partial_attention(own, sel, q_all, kv, late):
    n_keys = INNER * CH
    return pl.pallas_call(
        attention_kernel,
        out_shape=[jax.ShapeDtypeStruct((OUTER, HD + EXTRA, QC), jnp.bfloat16)] * 2,
        grid=(OUTER // PER,),
        in_specs=[
            pl.BlockSpec(memory_space=pltpu.SMEM),
            pl.BlockSpec(memory_space=pltpu.SMEM),
            pl.BlockSpec((PER, ROWS, HEADS * HD), lambda i: (i, 0, 0)),
            *[pl.BlockSpec((4 * ROWS, HD), lambda i: (0, 0)) for _ in range(FAR)],
            pl.BlockSpec((PER, 16, n_keys), lambda i: (i, 0, 0)),
        ],
        out_specs=[pl.BlockSpec((PER, HD + EXTRA, QC), lambda i: (i, 0, 0))] * 2,
        scratch_shapes=[
            pltpu.VMEM((INNER, 2, CH, 2 * HD), jnp.bfloat16),
            pltpu.VMEM((n_keys + CH, 2 * HD), jnp.bfloat16),
            pltpu.VMEM((HD, n_keys + CH), jnp.bfloat16),
            pltpu.VMEM((HD, n_keys), jnp.bfloat16),
            pltpu.VMEM((HD, n_keys), jnp.bfloat16),
        ],
        compiler_params=pltpu.CompilerParams(dimension_semantics=("arbitrary",)),
        cost_estimate=pl.CostEstimate(flops=8 * 10**9, bytes_accessed=6 * 10**6, transcendentals=5 * 10**6),
        name="partial_attention",
    )(own, sel, q_all, *kv, late)


def combine_kernel(part_ref, out_ref):
    lse = []
    for o in range(OUTER):
        terms = part_ref[o, HD:, :].astype(jnp.float32)
        lse.append(terms[0:1] + terms[1:2] + terms[2:3])
    top = lse[0]
    for o in range(1, OUTER):
        top = jnp.maximum(top, lse[o])
    total = jnp.zeros_like(top)
    acc = jnp.zeros((HD, QC), jnp.float32)
    for o in range(OUTER):
        w = jnp.exp2(lse[o] - top)
        total = total + w
        acc = acc + w * part_ref[o, :HD, :].astype(jnp.float32)
    mixed = (acc * (1.0 / total)).T
    heads = [mixed[h * CH : (h + 1) * CH] for h in range(HEADS)]
    out_ref[...] = jnp.concatenate(heads, axis=1).astype(jnp.bfloat16)


def combine(parts):
    return pl.pallas_call(
        combine_kernel,
        out_shape=jax.ShapeDtypeStruct((CH, HEADS * HD), jnp.bfloat16),
        in_specs=[pl.BlockSpec(memory_space=pltpu.VMEM)],
        out_specs=pl.BlockSpec(memory_space=pltpu.VMEM),
        cost_estimate=pl.CostEstimate(flops=10**8, bytes_accessed=12 * 10**5, transcendentals=0),
        name="combine",
    )(parts)


def project_kernel(place_ref, x_ref, y_ref, w_ref, v_ref, *outs):
    step = pl.program_id(0)
    got = dot(x_ref[...], w_ref[...], ((1,), (0,))) + dot(y_ref[...], v_ref[...], ((1,), (0,)))
    got = got.astype(jnp.bfloat16)
    for n, out in enumerate(outs):

        @pl.when(step == n)
        def _():
            out[...] = got


def project(place, x, y, w_own, w_other, hops, width):
    cuts = 2 * HALF // width

    def block(i, place_ref):
        hop = jnp.int32(hops[-1])
        for n in range(len(hops) - 1):
            hop = jnp.where(i // cuts == n, jnp.int32(hops[n]), hop)
        to = lax.rem(place_ref[0] + hop, ZHI)
        return (0, (2 * to + place_ref[1]) * cuts + lax.rem(i, cuts))

    rows, depth = x.shape
    count = cuts * len(hops)
    return pl.pallas_call(
        project_kernel,
        out_shape=[jax.ShapeDtypeStruct((rows, width), jnp.bfloat16)] * count,
        grid_spec=pltpu.PrefetchScalarGridSpec(
            num_scalar_prefetch=1,
            grid=(count,),
            in_specs=[
                pl.BlockSpec((rows, depth), lambda i, p: (0, 0)),
                pl.BlockSpec((rows, depth), lambda i, p: (0, 0)),
                pl.BlockSpec((depth, width), block),
                pl.BlockSpec((depth, width), block),
            ],
            out_specs=[pl.BlockSpec((rows, width), lambda i, p: (0, 0))] * count,
        ),
        compiler_params=pltpu.CompilerParams(dimension_semantics=("arbitrary",)),
        cost_estimate=pl.CostEstimate(
            flops=10 * 2 * rows * 2 * depth * width * count,
            bytes_accessed=2 * depth * width * count * 2,
            transcendentals=0,
        ),
        name="project",
    )(place, x, y, w_own, w_other)


def added(*terms):
    return sum(t.astype(jnp.float32) for t in terms).astype(jnp.bfloat16)


def xor_to(axis, size, mask, x):
    return lax.ppermute(x, axis, [(n, n ^ mask) for n in range(size)])


def shards(queries, keys, values, stretch_order, w_out):
    o = lax.axis_index("outer")
    i = lax.axis_index("inner")
    t = lax.axis_index("tensor")
    z, core = t // 2, t % 2
    place = jnp.stack([z, core]).astype(jnp.int32)

    q_many = jnp.broadcast_to(queries[None], (OUTER,) + queries.shape)
    q_all = lax.all_to_all(q_many, "outer", 0, 0, tiled=True)
    early = stretch_order.reshape(OUTER, INNER, 2)[:, :, 0]
    j = lax.dynamic_index_in_dim(early, i, 1, keepdims=False)
    k_row = lax.dynamic_index_in_dim(early, o, 0, keepdims=False)
    slots = jnp.arange(INNER, dtype=jnp.int32)
    hit = (slots[:, None] ^ i) == slots[None, :]
    k_here = jnp.sum(jnp.where(hit, k_row[None, :], 0), axis=1)
    late = (k_here[None, :] > j[:, None]).astype(jnp.int32)
    late_rows = jnp.broadcast_to(
        jnp.repeat(late, CH, axis=1).astype(jnp.bfloat16)[:, None, :], (OUTER, 16, INNER * CH)
    )

    kv_own = jnp.concatenate([keys, values], axis=0)
    kv_own = jnp.concatenate([kv_own, xor_to("inner", INNER, FAR, kv_own)], axis=0)
    kv_own, late, late_rows, place = lax.optimization_barrier((kv_own, late, late_rows, place))
    kv = [kv_own] + [xor_to("inner", INNER, s, kv_own) for s in range(1, FAR)]

    q_all, kv, w_send = lax.optimization_barrier((q_all, kv, w_out))
    w_other = xor_to("tensor", 2 * ZHI, 1, w_send)

    part_e, part_l = partial_attention(o.reshape(1), late.reshape(-1), q_all, kv, late_rows)
    part_e = lax.all_to_all(part_e, "outer", 0, 0, tiled=True)
    part_e, part_l = lax.optimization_barrier((part_e, part_l))
    part_l = lax.all_to_all(part_l, "outer", 0, 0, tiled=True)

    up = [(n, (n + 2) % (2 * ZHI)) for n in range(2 * ZHI)]
    down = [(n, (n - 2) % (2 * ZHI)) for n in range(2 * ZHI)]
    results = []
    for half in range(2):
        x = combine(part_l if half else part_e)
        y = xor_to("tensor", 2 * ZHI, 1, x)
        far_a, far_b = project(place, x, y, w_out, w_other, (2,), HALF)
        relay_a = lax.ppermute(far_a, "tensor", up)
        relay_b = lax.ppermute(far_b, "tensor", down)
        to_up, to_down, mine = project(place, x, y, w_out, w_other, (1, 3, 0), 2 * HALF)
        zero = jnp.zeros((), jnp.bfloat16)
        to_up = added(to_up, lax.pad(relay_a, zero, ((0, 0, 0), (0, HALF, 0))))
        to_down = added(to_down, lax.pad(relay_b, zero, ((0, 0, 0), (HALF, 0, 0))))
        if half == 0:
            part_l, to_up, to_down = lax.optimization_barrier((part_l, to_up, to_down))
        below = lax.ppermute(to_up, "tensor", up)
        above = lax.ppermute(to_down, "tensor", down)
        results.append(added(mine, below, above))
    return jnp.concatenate(results, axis=0)


def solution(mesh):
    placed = (
        P(("outer", "inner"), "tensor"),
        P(("outer", "inner"), "tensor"),
        P(("outer", "inner"), "tensor"),
        P(),
        P("tensor", None),
    )
    return jax.shard_map(
        shards,
        mesh=mesh,
        in_specs=placed,
        out_specs=P(("outer", "inner"), "tensor"),
        check_vma=False,
    )
```

profile of v0, /device:TPU:103, one launch (start us, length us, event | category | flops | bytes accessed | tf_op | source)
XLA Modules:
  0.0 229.1 jit_solution(6359922528809342641)
XLA Ops:
  0.0 2.5 %broadcast_in_dim.39 = bf16[16,128,512]{2,1,0:T(8,128)(2,1)} broadcast(bf16[128,512]{1,0:T(8,128)(2,1)} %param.5), dimensions={1,2} | broadcast | bytes 2228224 | tf_op jit(solution)/shard_map/broadcast_in_dim | solution.py:246
  2.5 7.0 %all-to-all-start = ((bf16[16,128,512]{2,1,0:T(8,128)(2,1)}), bf16[16,128,512]{2,1,0:T(8,128)(2,1)S(1)}, u32[]{:S(2)}, u32[]{:S(2)}) async-start(bf16[16,128,512]{2,1,0:T(8,128)(2,1)} %broadcast_in_dim.39), calls=%async_computation | async-start | bytes 4194304 | tf_op jit(solution)/shard_map/all_to_all | solution.py:247
  9.5 8.8 %collective-permute-start = (bf16[256,128]{1,0:T(8,128)(2,1)S(1)}, bf16[256,128]{1,0:T(8,128)(2,1)S(1)}, u32[]{:S(2)}, u32[]{:S(2)}) collective-permute-start(bf16[256,128]{1,0:T(8,128)(2,1)S(1)} %pad_maximum_fusion.2), channel_id=1, source_target_pairs={{0,32},{8,40},{16,48},{24,56},{32,0},{40,8},{48,16},{56,24},{1,33}... | collective-permute-start | bytes 196616 | tf_op jit(solution)/shard_map/ppermute | solution.py:236
  20.1 2.7 %collective-permute-done = bf16[256,128]{1,0:T(8,128)(2,1)S(1)} collective-permute-done((bf16[256,128]{1,0:T(8,128)(2,1)S(1)}, bf16[256,128]{1,0:T(8,128)(2,1)S(1)}, u32[]{:S(2)}, u32[]{:S(2)}) %collective-permute-start) | collective-permute-done | bytes 65568 | tf_op jit(solution)/shard_map/ppermute | solution.py:236
  23.6 1.9 collective-permute-start.3
  25.5 1.9 collective-permute-start.2
  27.4 5.4 %collective-permute-start.1 = (bf16[512,128]{1,0:T(8,128)(2,1)S(1)}, bf16[512,128]{1,0:T(8,128)(2,1)S(1)}, u32[]{:S(2)}, u32[]{:S(2)}) collective-permute-start(bf16[512,128]{1,0:T(8,128)(2,1)S(1)} %pad_maximum_fusion.1.refs_0_), channel_id=1, source_target_pairs={{0,8},{8,0},{16,24},{24,16},{32,40},{40,32},{48,56},{56,48},{1,9},... | collective-permute-start | bytes 393224 | tf_op jit(solution)/shard_map/ppermute | solution.py:236
  32.9 2.9 %collective-permute-done.2.refs_2_ = bf16[512,128]{1,0:T(8,128)(2,1)S(1)} collective-permute-done((bf16[512,128]{1,0:T(8,128)(2,1)S(1)}, bf16[512,128]{1,0:T(8,128)(2,1)S(1)}, u32[]{:S(2)}, u32[]{:S(2)}) %collective-permute-start.2) | collective-permute-done | bytes 131104 | tf_op jit(solution)/shard_map/ppermute | solution.py:236
  37.0 6.0 %collective-permute-start.5 = (bf16[512,8192]{1,0:T(8,128)(2,1)}, bf16[512,8192]{1,0:T(8,128)(2,1)}, u32[]{:S(2)}, u32[]{:S(2)}) collective-permute-start(bf16[512,8192]{1,0:T(8,128)(2,1)} %w_ref.7), channel_id=1, source_target_pairs={{0,1},{1,0},{2,3},{3,2},{4,5},{5,4},{6,7},{7,6},{8,9},{9,8},{10,11... | collective-permute-start | bytes 25165832 | tf_op jit(solution)/shard_map/ppermute | solution.py:236
  43.7 13.8 %partial_attention.1 = (bf16[16,144,256]{2,1,0:T(8,128)(2,1)}, bf16[16,144,256]{2,1,0:T(8,128)(2,1)}) custom-call(s32[1]{0:T(128)} %bitcast.2.own_ref, s32[128]{0:T(128)} %reshape.29.sel_ref, bf16[16,128,512]{2,1,0:T(8,128)(2,1)} %copy-done.1, bf16[512,128]{1,0:T(8,128)(2,1)} %copy-done.4, bf16[512,128]{1,0:T(8,128)(2,1)} %copy-done.11, ...), custom_call_target="tpu_custom_call" | custom-call | flops 8000000000 | bytes 6000000 | tf_op jit(solution)/shard_map/partial_attention/pallas_call | solution.py:129
  57.5 23.1 %all_to_all.15.part_ref = bf16[16,144,256]{2,1,0:T(8,128)(2,1)} all-to-all(bf16[16,144,256]{2,1,0:T(8,128)(2,1)} %get-tuple-element.41), channel_id=1, replica_groups=mesh['outer'=16,'inner'=8,'tensor'=8] {'outer'}, dimensions={0} | all-to-all | bytes 2359296 | tf_op jit(solution)/shard_map/all_to_all | solution.py:268
  80.6 5.3 %all-to-all-start.2 = ((bf16[16,144,256]{2,1,0:T(8,128)(2,1)}), bf16[16,144,256]{2,1,0:T(8,128)(2,1)S(1)}, u32[]{:S(2)}, u32[]{:S(2)}) async-start(bf16[16,144,256]{2,1,0:T(8,128)(2,1)} %get-tuple-element.46), calls=%async_computation.2 | async-start | bytes 2359296 | tf_op jit(solution)/shard_map/all_to_all | solution.py:270
  85.9 2.2 combine.2.x_ref
  88.1 3.5 %collective-permute-start.4 = (bf16[64,512]{1,0:T(8,128)(2,1)}, bf16[64,512]{1,0:T(8,128)(2,1)S(1)}, u32[]{:S(2)}, u32[]{:S(2)}) collective-permute-start(bf16[64,512]{1,0:T(8,128)(2,1)} %combine.2.x_ref), channel_id=1, source_target_pairs={{0,1},{1,0},{2,3},{3,2},{4,5},{5,4},{6,7},{7,6},{8,9},{9,8},{10,11... | collective-permute-start | bytes 196616 | tf_op jit(solution)/shard_map/ppermute | solution.py:236
  93.4 3.2 %project.5 = (bf16[64,512]{1,0:T(8,128)(2,1)}, bf16[64,512]{1,0:T(8,128)(2,1)}) custom-call(s32[2]{0:T(128)} %pad_add_fusion.place_ref, bf16[64,512]{1,0:T(8,128)(2,1)} %combine.2.x_ref, bf16[64,512]{1,0:T(8,128)(2,1)} %copy-done.3, bf16[512,8192]{1,0:T(8,128)(2,1)} %w_ref.7, bf16[512,8192]{1,0:T(8,128)(2,1)} %collective-permute-done.5.v_ref), custom_call_target="tpu_custom_call" | custom-call | flops 1342177280 | bytes 2097152 | tf_op jit(solution)/shard_map/project/pallas_call | solution.py:207
  96.6 14.4 %collective-permute-start.6 = (bf16[64,512]{1,0:T(8,128)(2,1)}, bf16[64,512]{1,0:T(8,128)(2,1)S(1)}, u32[]{:S(2)}, u32[]{:S(2)}) collective-permute-start(bf16[64,512]{1,0:T(8,128)(2,1)} %get-tuple-element.48), channel_id=1, source_target_pairs={{0,2},{1,3},{2,4},{3,5},{4,6},{5,7},{6,0},{7,1},{8,10},{9,11},{10,... | collective-permute-start | bytes 196616 | tf_op jit(solution)/shard_map/ppermute | solution.py:279
  111.0 6.4 %collective-permute-start.7 = (bf16[64,512]{1,0:T(8,128)(2,1)}, bf16[64,512]{1,0:T(8,128)(2,1)S(1)}, u32[]{:S(2)}, u32[]{:S(2)}) collective-permute-start(bf16[64,512]{1,0:T(8,128)(2,1)} %get-tuple-element.50), channel_id=1, source_target_pairs={{0,6},{1,7},{2,0},{3,1},{4,2},{5,3},{6,4},{7,5},{8,14},{9,15},{10,... | collective-permute-start | bytes 196616 | tf_op jit(solution)/shard_map/ppermute | solution.py:280
  117.4 5.6 %project.4 = (bf16[64,1024]{1,0:T(8,128)(2,1)}, bf16[64,1024]{1,0:T(8,128)(2,1)}, bf16[64,1024]{1,0:T(8,128)(2,1)}) custom-call(s32[2]{0:T(128)} %pad_add_fusion.place_ref, bf16[64,512]{1,0:T(8,128)(2,1)} %combine.2.x_ref, bf16[64,512]{1,0:T(8,128)(2,1)} %copy-done.3, bf16[512,8192]{1,0:T(8,128)(2,1)} %w_ref.7, bf16[512,8192]{1,0:T(8,128)(2,1)} %collective-permute-done.5.v_ref), custom_call_target="tpu_custom_call" | custom-call | flops 4026531840 | bytes 6291456 | tf_op jit(solution)/shard_map/project/pallas_call | solution.py:207
  123.9 1.7 collective-permute-done.7
  127.6 2.2 combine.3.x_ref
  129.9 3.4 %collective-permute-start.10 = (bf16[64,512]{1,0:T(8,128)(2,1)}, bf16[64,512]{1,0:T(8,128)(2,1)S(1)}, u32[]{:S(2)}, u32[]{:S(2)}) collective-permute-start(bf16[64,512]{1,0:T(8,128)(2,1)} %combine.3.x_ref), channel_id=1, source_target_pairs={{0,1},{1,0},{2,3},{3,2},{4,5},{5,4},{6,7},{7,6},{8,9},{9,8},{10,11... | collective-permute-start | bytes 196616 | tf_op jit(solution)/shard_map/ppermute | solution.py:236
  133.2 20.2 %collective-permute-start.8 = (bf16[64,1024]{1,0:T(8,128)(2,1)S(1)}, bf16[64,1024]{1,0:T(8,128)(2,1)S(1)}, u32[]{:S(2)}, u32[]{:S(2)}) collective-permute-start(bf16[64,1024]{1,0:T(8,128)(2,1)S(1)} %add_convert_fusion.5), channel_id=1, source_target_pairs={{0,2},{1,3},{2,4},{3,5},{4,6},{5,7},{6,0},{7,1},{8,10},{9,11},{10,... | collective-permute-start | bytes 393224 | tf_op jit(solution)/shard_map/ppermute | solution.py:287
  153.5 1.9 collective-permute-start.9
  156.0 3.2 %project.7 = (bf16[64,512]{1,0:T(8,128)(2,1)}, bf16[64,512]{1,0:T(8,128)(2,1)}) custom-call(s32[2]{0:T(128)} %pad_add_fusion.place_ref, bf16[64,512]{1,0:T(8,128)(2,1)} %combine.3.x_ref, bf16[64,512]{1,0:T(8,128)(2,1)} %copy-done.2, bf16[512,8192]{1,0:T(8,128)(2,1)} %w_ref.7, bf16[512,8192]{1,0:T(8,128)(2,1)} %collective-permute-done.5.v_ref), custom_call_target="tpu_custom_call" | custom-call | flops 1342177280 | bytes 2097152 | tf_op jit(solution)/shard_map/project/pallas_call | solution.py:207
  159.3 12.1 %collective-permute-start.11 = (bf16[64,512]{1,0:T(8,128)(2,1)}, bf16[64,512]{1,0:T(8,128)(2,1)S(1)}, u32[]{:S(2)}, u32[]{:S(2)}) collective-permute-start(bf16[64,512]{1,0:T(8,128)(2,1)} %get-tuple-element.56), channel_id=1, source_target_pairs={{0,2},{1,3},{2,4},{3,5},{4,6},{5,7},{6,0},{7,1},{8,10},{9,11},{10,... | collective-permute-start | bytes 196616 | tf_op jit(solution)/shard_map/ppermute | solution.py:279
  171.3 2.1 collective-permute-start.13
  173.4 5.6 %project.6 = (bf16[64,1024]{1,0:T(8,128)(2,1)}, bf16[64,1024]{1,0:T(8,128)(2,1)}, bf16[64,1024]{1,0:T(8,128)(2,1)}) custom-call(s32[2]{0:T(128)} %pad_add_fusion.place_ref, bf16[64,512]{1,0:T(8,128)(2,1)} %combine.3.x_ref, bf16[64,512]{1,0:T(8,128)(2,1)} %copy-done.2, bf16[512,8192]{1,0:T(8,128)(2,1)} %w_ref.7, bf16[512,8192]{1,0:T(8,128)(2,1)} %collective-permute-done.5.v_ref), custom_call_target="tpu_custom_call" | custom-call | flops 4026531840 | bytes 6291456 | tf_op jit(solution)/shard_map/project/pallas_call | solution.py:207
  179.0 18.4 %collective-permute-done.13 = bf16[64,512]{1,0:T(8,128)(2,1)S(1)} collective-permute-done((bf16[64,512]{1,0:T(8,128)(2,1)}, bf16[64,512]{1,0:T(8,128)(2,1)S(1)}, u32[]{:S(2)}, u32[]{:S(2)}) %collective-permute-start.13) | collective-permute-done | bytes 65568 | tf_op jit(solution)/shard_map/ppermute | solution.py:280
  198.3 5.8 %collective-permute-start.14 = (bf16[64,1024]{1,0:T(8,128)(2,1)S(1)}, bf16[64,1024]{1,0:T(8,128)(2,1)S(1)}, u32[]{:S(2)}, u32[]{:S(2)}) collective-permute-start(bf16[64,1024]{1,0:T(8,128)(2,1)S(1)} %add_convert_fusion.1), channel_id=1, source_target_pairs={{0,6},{1,7},{2,0},{3,1},{4,2},{5,3},{6,4},{7,5},{8,14},{9,15},{10,... | collective-permute-start | bytes 393224 | tf_op jit(solution)/shard_map/ppermute | solution.py:288
  205.0 8.2 %collective-permute-start.12 = (bf16[64,1024]{1,0:T(8,128)(2,1)S(1)}, bf16[64,1024]{1,0:T(8,128)(2,1)S(1)}, u32[]{:S(2)}, u32[]{:S(2)}) collective-permute-start(bf16[64,1024]{1,0:T(8,128)(2,1)S(1)} %add_convert_fusion.2), channel_id=1, source_target_pairs={{0,2},{1,3},{2,4},{3,5},{4,6},{5,7},{6,0},{7,1},{8,10},{9,11},{10,... | collective-permute-start | bytes 393224 | tf_op jit(solution)/shard_map/ppermute | solution.py:287
  213.4 8.6 %collective-permute-done.14 = bf16[64,1024]{1,0:T(8,128)(2,1)S(1)} collective-permute-done((bf16[64,1024]{1,0:T(8,128)(2,1)S(1)}, bf16[64,1024]{1,0:T(8,128)(2,1)S(1)}, u32[]{:S(2)}, u32[]{:S(2)}) %collective-permute-start.14) | collective-permute-done | bytes 131104 | tf_op jit(solution)/shard_map/ppermute | solution.py:288
  221.9 5.5 %collective-permute-done.12 = bf16[64,1024]{1,0:T(8,128)(2,1)S(1)} collective-permute-done((bf16[64,1024]{1,0:T(8,128)(2,1)S(1)}, bf16[64,1024]{1,0:T(8,128)(2,1)S(1)}, u32[]{:S(2)}, u32[]{:S(2)}) %collective-permute-start.12) | collective-permute-done | bytes 131104 | tf_op jit(solution)/shard_map/ppermute | solution.py:287
  (55 shorter events, 13.3 us)
Async XLA Ops:
  2.5 7.0 %copy-start.6 = (bf16[128,128]{1,0:T(8,128)(2,1)S(1)}, bf16[128,128]{1,0:T(8,128)(2,1)}, u32[]{:S(2)}) copy-start(bf16[128,128]{1,0:T(8,128)(2,1)} %param.7) | copy-start | bytes 98308
  2.5 7.0 %copy-start.7 = (bf16[128,128]{1,0:T(8,128)(2,1)S(1)}, bf16[128,128]{1,0:T(8,128)(2,1)}, u32[]{:S(2)}) copy-start(bf16[128,128]{1,0:T(8,128)(2,1)} %param.6) | copy-start | bytes 98308
  2.5 15.9 %copy-start.8 = (s32[256]{0:T(256)S(1)}, s32[256]{0:T(256)}, u32[]{:S(2)}) copy-start(s32[256]{0:T(256)} %param.8) | copy-start | bytes 3076
  2.5 34.5 %all-to-all-start = ((bf16[16,128,512]{2,1,0:T(8,128)(2,1)}), bf16[16,128,512]{2,1,0:T(8,128)(2,1)S(1)}, u32[]{:S(2)}, u32[]{:S(2)}) async-start(bf16[16,128,512]{2,1,0:T(8,128)(2,1)} %broadcast_in_dim.39), calls=%async_computation | async-start | bytes 4194304 | tf_op jit(solution)/shard_map/all_to_all | solution.py:247
  9.5 13.3 %collective-permute-start = (bf16[256,128]{1,0:T(8,128)(2,1)S(1)}, bf16[256,128]{1,0:T(8,128)(2,1)S(1)}, u32[]{:S(2)}, u32[]{:S(2)}) collective-permute-start(bf16[256,128]{1,0:T(8,128)(2,1)S(1)} %pad_maximum_fusion.2), channel_id=1, source_target_pairs={{0,32},{8,40},{16,48},{24,56},{32,0},{40,8},{48,16},{56,24},{1,33}... | collective-permute-start | bytes 196616 | tf_op jit(solution)/shard_map/ppermute | solution.py:236
  22.8 20.9 %copy-start.4 = (bf16[512,128]{1,0:T(8,128)(2,1)}, bf16[512,128]{1,0:T(8,128)(2,1)S(1)}, u32[]{:S(2)}) copy-start(bf16[512,128]{1,0:T(8,128)(2,1)S(1)} %pad_maximum_fusion.1.refs_0_) | copy-start | bytes 393220
  23.6 9.3 %collective-permute-start.3 = (bf16[512,128]{1,0:T(8,128)(2,1)S(1)}, bf16[512,128]{1,0:T(8,128)(2,1)S(1)}, u32[]{:S(2)}, u32[]{:S(2)}) collective-permute-start(bf16[512,128]{1,0:T(8,128)(2,1)S(1)} %pad_maximum_fusion.1.refs_0_), channel_id=1, source_target_pairs={{0,24},{8,16},{16,8},{24,0},{32,56},{40,48},{48,40},{56,32},{1,25}... | collective-permute-start | bytes 393224 | tf_op jit(solution)/shard_map/ppermute | solution.py:236
  25.5 10.3 %collective-permute-start.2 = (bf16[512,128]{1,0:T(8,128)(2,1)S(1)}, bf16[512,128]{1,0:T(8,128)(2,1)S(1)}, u32[]{:S(2)}, u32[]{:S(2)}) collective-permute-start(bf16[512,128]{1,0:T(8,128)(2,1)S(1)} %pad_maximum_fusion.1.refs_0_), channel_id=1, source_target_pairs={{0,16},{8,24},{16,0},{24,8},{32,48},{40,56},{48,32},{56,40},{1,17}... | collective-permute-start | bytes 393224 | tf_op jit(solution)/shard_map/ppermute | solution.py:236
  27.4 9.6 %collective-permute-start.1 = (bf16[512,128]{1,0:T(8,128)(2,1)S(1)}, bf16[512,128]{1,0:T(8,128)(2,1)S(1)}, u32[]{:S(2)}, u32[]{:S(2)}) collective-permute-start(bf16[512,128]{1,0:T(8,128)(2,1)S(1)} %pad_maximum_fusion.1.refs_0_), channel_id=1, source_target_pairs={{0,8},{8,0},{16,24},{24,16},{32,40},{40,32},{48,56},{56,48},{1,9},... | collective-permute-start | bytes 393224 | tf_op jit(solution)/shard_map/ppermute | solution.py:236
  32.9 10.8 %copy-start.9 = (bf16[512,128]{1,0:T(8,128)(2,1)}, bf16[512,128]{1,0:T(8,128)(2,1)S(1)}, u32[]{:S(2)}) copy-start(bf16[512,128]{1,0:T(8,128)(2,1)S(1)} %collective-permute-done.3.refs_3_) | copy-start | bytes 393220
  35.8 7.9 %copy-start.10 = (bf16[512,128]{1,0:T(8,128)(2,1)}, bf16[512,128]{1,0:T(8,128)(2,1)S(1)}, u32[]{:S(2)}) copy-start(bf16[512,128]{1,0:T(8,128)(2,1)S(1)} %collective-permute-done.2.refs_2_) | copy-start | bytes 393220
  37.0 6.7 %copy-start.11 = (bf16[512,128]{1,0:T(8,128)(2,1)}, bf16[512,128]{1,0:T(8,128)(2,1)S(1)}, u32[]{:S(2)}) copy-start(bf16[512,128]{1,0:T(8,128)(2,1)S(1)} %collective-permute-done.1.refs_1_) | copy-start | bytes 393220
  37.0 6.7 %copy-start.1 = (bf16[16,128,512]{2,1,0:T(8,128)(2,1)}, bf16[16,128,512]{2,1,0:T(8,128)(2,1)S(1)}, u32[]{:S(2)}) copy-start(bf16[16,128,512]{2,1,0:T(8,128)(2,1)S(1)} %all-to-all-done.q_ref) | copy-start | bytes 6291460
  37.0 55.8 %collective-permute-start.5 = (bf16[512,8192]{1,0:T(8,128)(2,1)}, bf16[512,8192]{1,0:T(8,128)(2,1)}, u32[]{:S(2)}, u32[]{:S(2)}) collective-permute-start(bf16[512,8192]{1,0:T(8,128)(2,1)} %w_ref.7), channel_id=1, source_target_pairs={{0,1},{1,0},{2,3},{3,2},{4,5},{5,4},{6,7},{7,6},{8,9},{9,8},{10,11... | collective-permute-start | bytes 25165832 | tf_op jit(solution)/shard_map/ppermute | solution.py:236
  80.6 45.9 %all-to-all-start.2 = ((bf16[16,144,256]{2,1,0:T(8,128)(2,1)}), bf16[16,144,256]{2,1,0:T(8,128)(2,1)S(1)}, u32[]{:S(2)}, u32[]{:S(2)}) async-start(bf16[16,144,256]{2,1,0:T(8,128)(2,1)} %get-tuple-element.46), calls=%async_computation.2 | async-start | bytes 2359296 | tf_op jit(solution)/shard_map/all_to_all | solution.py:270
  88.1 4.6 %collective-permute-start.4 = (bf16[64,512]{1,0:T(8,128)(2,1)}, bf16[64,512]{1,0:T(8,128)(2,1)S(1)}, u32[]{:S(2)}, u32[]{:S(2)}) collective-permute-start(bf16[64,512]{1,0:T(8,128)(2,1)} %combine.2.x_ref), channel_id=1, source_target_pairs={{0,1},{1,0},{2,3},{3,2},{4,5},{5,4},{6,7},{7,6},{8,9},{9,8},{10,11... | collective-permute-start | bytes 196616 | tf_op jit(solution)/shard_map/ppermute | solution.py:236
  92.8 0.6 copy-start.3
  96.6 26.4 %collective-permute-start.6 = (bf16[64,512]{1,0:T(8,128)(2,1)}, bf16[64,512]{1,0:T(8,128)(2,1)S(1)}, u32[]{:S(2)}, u32[]{:S(2)}) collective-permute-start(bf16[64,512]{1,0:T(8,128)(2,1)} %get-tuple-element.48), channel_id=1, source_target_pairs={{0,2},{1,3},{2,4},{3,5},{4,6},{5,7},{6,0},{7,1},{8,10},{9,11},{10,... | collective-permute-start | bytes 196616 | tf_op jit(solution)/shard_map/ppermute | solution.py:279
  111.0 14.6 %collective-permute-start.7 = (bf16[64,512]{1,0:T(8,128)(2,1)}, bf16[64,512]{1,0:T(8,128)(2,1)S(1)}, u32[]{:S(2)}, u32[]{:S(2)}) collective-permute-start(bf16[64,512]{1,0:T(8,128)(2,1)} %get-tuple-element.50), channel_id=1, source_target_pairs={{0,6},{1,7},{2,0},{3,1},{4,2},{5,3},{6,4},{7,5},{8,14},{9,15},{10,... | collective-permute-start | bytes 196616 | tf_op jit(solution)/shard_map/ppermute | solution.py:280
  126.5 1.1 copy-start
  129.9 25.5 %collective-permute-start.10 = (bf16[64,512]{1,0:T(8,128)(2,1)}, bf16[64,512]{1,0:T(8,128)(2,1)S(1)}, u32[]{:S(2)}, u32[]{:S(2)}) collective-permute-start(bf16[64,512]{1,0:T(8,128)(2,1)} %combine.3.x_ref), channel_id=1, source_target_pairs={{0,1},{1,0},{2,3},{3,2},{4,5},{5,4},{6,7},{7,6},{8,9},{9,8},{10,11... | collective-permute-start | bytes 196616 | tf_op jit(solution)/shard_map/ppermute | solution.py:236
  133.2 80.0 %collective-permute-start.8 = (bf16[64,1024]{1,0:T(8,128)(2,1)S(1)}, bf16[64,1024]{1,0:T(8,128)(2,1)S(1)}, u32[]{:S(2)}, u32[]{:S(2)}) collective-permute-start(bf16[64,1024]{1,0:T(8,128)(2,1)S(1)} %add_convert_fusion.5), channel_id=1, source_target_pairs={{0,2},{1,3},{2,4},{3,5},{4,6},{5,7},{6,0},{7,1},{8,10},{9,11},{10,... | collective-permute-start | bytes 393224 | tf_op jit(solution)/shard_map/ppermute | solution.py:287
  153.5 59.8 %collective-permute-start.9 = (bf16[64,1024]{1,0:T(8,128)(2,1)S(1)}, bf16[64,1024]{1,0:T(8,128)(2,1)S(1)}, u32[]{:S(2)}, u32[]{:S(2)}) collective-permute-start(bf16[64,1024]{1,0:T(8,128)(2,1)S(1)} %add_convert_fusion.4), channel_id=1, source_target_pairs={{0,6},{1,7},{2,0},{3,1},{4,2},{5,3},{6,4},{7,5},{8,14},{9,15},{10,... | collective-permute-start | bytes 393224 | tf_op jit(solution)/shard_map/ppermute | solution.py:288
  155.4 0.6 copy-start.2
  159.3 44.8 %collective-permute-start.11 = (bf16[64,512]{1,0:T(8,128)(2,1)}, bf16[64,512]{1,0:T(8,128)(2,1)S(1)}, u32[]{:S(2)}, u32[]{:S(2)}) collective-permute-start(bf16[64,512]{1,0:T(8,128)(2,1)} %get-tuple-element.56), channel_id=1, source_target_pairs={{0,2},{1,3},{2,4},{3,5},{4,6},{5,7},{6,0},{7,1},{8,10},{9,11},{10,... | collective-permute-start | bytes 196616 | tf_op jit(solution)/shard_map/ppermute | solution.py:279
  171.3 42.0 %copy-start.5 = (bf16[64,1024]{1,0:T(8,128)(2,1)S(1)}, bf16[64,1024]{1,0:T(8,128)(2,1)}, u32[]{:S(2)}) copy-start(bf16[64,1024]{1,0:T(8,128)(2,1)} %get-tuple-element.45) | copy-start | bytes 393220
  171.3 26.1 %collective-permute-start.13 = (bf16[64,512]{1,0:T(8,128)(2,1)}, bf16[64,512]{1,0:T(8,128)(2,1)S(1)}, u32[]{:S(2)}, u32[]{:S(2)}) collective-permute-start(bf16[64,512]{1,0:T(8,128)(2,1)} %get-tuple-element.58), channel_id=1, source_target_pairs={{0,6},{1,7},{2,0},{3,1},{4,2},{5,3},{6,4},{7,5},{8,14},{9,15},{10,... | collective-permute-start | bytes 196616 | tf_op jit(solution)/shard_map/ppermute | solution.py:280
  198.3 23.6 %collective-permute-start.14 = (bf16[64,1024]{1,0:T(8,128)(2,1)S(1)}, bf16[64,1024]{1,0:T(8,128)(2,1)S(1)}, u32[]{:S(2)}, u32[]{:S(2)}) collective-permute-start(bf16[64,1024]{1,0:T(8,128)(2,1)S(1)} %add_convert_fusion.1), channel_id=1, source_target_pairs={{0,6},{1,7},{2,0},{3,1},{4,2},{5,3},{6,4},{7,5},{8,14},{9,15},{10,... | collective-permute-start | bytes 393224 | tf_op jit(solution)/shard_map/ppermute | solution.py:288
  205.0 22.4 %collective-permute-start.12 = (bf16[64,1024]{1,0:T(8,128)(2,1)S(1)}, bf16[64,1024]{1,0:T(8,128)(2,1)S(1)}, u32[]{:S(2)}, u32[]{:S(2)}) collective-permute-start(bf16[64,1024]{1,0:T(8,128)(2,1)S(1)} %add_convert_fusion.2), channel_id=1, source_target_pairs={{0,2},{1,3},{2,4},{3,5},{4,6},{5,7},{6,0},{7,1},{8,10},{9,11},{10,... | collective-permute-start | bytes 393224 | tf_op jit(solution)/shard_map/ppermute | solution.py:287
where the time goes:
time: 230 us; the launch traced here: 229 us
  starting transfers between devices  114 us (50%)
  waiting for transfers between devices  42.1 us (18%)
  Pallas kernels  35.9 us (16%)
  blocking collectives  23.1 us (10%)
  local copies, waits for them, and re-layouts  7.06 us (3%)
  other arithmetic  6.38 us (3%)
    ppermute x7, starting transfers between devices, xor_to(): return lax.ppermute(x, axis, [(n, n ^ mask) for n in range(size)])  31 us
    ppermute x2, starting transfers between devices, shards(): below = lax.ppermute(to_up, 'tensor', up)  28.4 us
    ppermute x2, starting transfers between devices, shards(): relay_a = lax.ppermute(far_a, 'tensor', up)  26.5 us
    all_to_all x1, blocking collectives, shards(): part_e = lax.all_to_all(part_e, 'outer', 0, 0, tiled=True)  23.1 us
    ppermute x2, waiting for transfers between devices, shards(): relay_b = lax.ppermute(far_b, 'tensor', down)  20.1 us
    pallas_call x4, Pallas kernels, project(): pl.pallas_call(project_kernel, out_shape=[jax.ShapeDtypeStruct((rows, wid...  17.6 us
    pallas_call x1, Pallas kernels, partial_attention(): pl.pallas_call(attention_kernel, out_shape=[jax.ShapeDtypeStruct((OUTER,...  13.8 us
    ppermute x2, waiting for transfers between devices, shards(): above = lax.ppermute(to_down, 'tensor', down)  8.56 us
  transfers between devices with their start and end apart: 17, of which 8 were waited for; matrix products, arithmetic and copies ran while one was open for 3% of the time, Pallas kernels for 15%

commit v1 on v0

--- a/solution.py
+++ b/solution.py
@@ -16,11 +16,12 @@
 INNER = 8
 FAR = 4
 ZHI = 4
-QC = HEADS * CH
+GROUP = 2
+QC = GROUP * CH
 EXTRA = 16
 NEG = -1e30
 COEF = math.log2(math.e) / math.sqrt(HD)
-PER = 2
+PER = 4
 HALF = 512
 
 
@@ -38,7 +39,7 @@
 
 def attention_kernel(own_ref, sel_ref, q_ref, *refs):
     pairs = refs[:FAR]
-    late_ref, oe_ref, ol_ref, pick, dense, vt_dense, vt_e, vt_l = refs[FAR:]
+    late_ref, out_ref, pick, dense, vt_dense, vt_e, vt_l = refs[FAR:]
 
     def rows_of(s, at):
         first = (s // FAR) * 2 * ROWS + at
@@ -75,7 +76,7 @@
         own = a == own_ref[0]
         q = q_ref[p]
         stacked = [
-            jnp.concatenate([q[r : r + CH, h * HD : (h + 1) * HD] for h in range(HEADS)], axis=0)
+            jnp.concatenate([q[r : r + CH, h * HD : (h + 1) * HD] for h in range(GROUP)], axis=0)
             for r in (0, CH)
         ]
         q_cat = jnp.concatenate(stacked, axis=1)
@@ -118,26 +119,26 @@
         inv_e = jnp.where(some, 1.0 / jnp.where(some, l_e, 1.0), 0.0)
         lse_e = jnp.where(some, m_e * COEF + jnp.log2(jnp.where(some, l_e, 1.0)), NEG)
         lse_l = m_l * COEF + jnp.log2(l_l)
-        for ref, o_t, inv, lse in ((oe_ref, o_e, inv_e, lse_e), (ol_ref, o_l, 1.0 / l_l, lse_l)):
-            ref[p, :HD, :] = (o_t * inv).astype(jnp.bfloat16)
+        for at, o_t, inv, lse in ((0, o_e, inv_e, lse_e), (QC, o_l, 1.0 / l_l, lse_l)):
             rows = list(three_terms(lse)) + [jnp.zeros((EXTRA - 3, QC), jnp.float32)]
-            ref[p, HD:, :] = jnp.concatenate(rows, axis=0).astype(jnp.bfloat16)
-
-
-def partial_attention(own, sel, q_all, kv, late):
+            out_ref[p, :HD, at : at + QC] = (o_t * inv).astype(jnp.bfloat16)
+            out_ref[p, HD:, at : at + QC] = jnp.concatenate(rows, axis=0).astype(jnp.bfloat16)
+
+
+def partial_attention(own, sel, q_all, kv, late, group):
     n_keys = INNER * CH
     return pl.pallas_call(
         attention_kernel,
-        out_shape=[jax.ShapeDtypeStruct((OUTER, HD + EXTRA, QC), jnp.bfloat16)] * 2,
+        out_shape=jax.ShapeDtypeStruct((OUTER, HD + EXTRA, 2 * QC), jnp.bfloat16),
         grid=(OUTER // PER,),
         in_specs=[
             pl.BlockSpec(memory_space=pltpu.SMEM),
             pl.BlockSpec(memory_space=pltpu.SMEM),
-            pl.BlockSpec((PER, ROWS, HEADS * HD), lambda i: (i, 0, 0)),
+            pl.BlockSpec((PER, ROWS, GROUP * HD), lambda i: (i, 0, group)),
             *[pl.BlockSpec((4 * ROWS, HD), lambda i: (0, 0)) for _ in range(FAR)],
             pl.BlockSpec((PER, 16, n_keys), lambda i: (i, 0, 0)),
         ],
-        out_specs=[pl.BlockSpec((PER, HD + EXTRA, QC), lambda i: (i, 0, 0))] * 2,
+        out_specs=pl.BlockSpec((PER, HD + EXTRA, 2 * QC), lambda i: (i, 0, 0)),
         scratch_shapes=[
             pltpu.VMEM((INNER, 2, CH, 2 * HD), jnp.bfloat16),
             pltpu.VMEM((n_keys + CH, 2 * HD), jnp.bfloat16),
@@ -146,7 +147,7 @@
             pltpu.VMEM((HD, n_keys), jnp.bfloat16),
         ],
         compiler_params=pltpu.CompilerParams(dimension_semantics=("arbitrary",)),
-        cost_estimate=pl.CostEstimate(flops=8 * 10**9, bytes_accessed=6 * 10**6, transcendentals=5 * 10**6),
+        cost_estimate=pl.CostEstimate(flops=4 * 10**9, bytes_accessed=3 * 10**6, transcendentals=2 * 10**6),
         name="partial_attention",
     )(own, sel, q_all, *kv, late)
 
@@ -160,20 +161,23 @@
     for o in range(1, OUTER):
         top = jnp.maximum(top, lse[o])
     total = jnp.zeros_like(top)
-    acc = jnp.zeros((HD, QC), jnp.float32)
+    acc = jnp.zeros((HD, 2 * QC), jnp.float32)
     for o in range(OUTER):
         w = jnp.exp2(lse[o] - top)
         total = total + w
         acc = acc + w * part_ref[o, :HD, :].astype(jnp.float32)
     mixed = (acc * (1.0 / total)).T
-    heads = [mixed[h * CH : (h + 1) * CH] for h in range(HEADS)]
-    out_ref[...] = jnp.concatenate(heads, axis=1).astype(jnp.bfloat16)
+    halves = []
+    for at in (0, QC):
+        heads = [mixed[at + h * CH : at + (h + 1) * CH] for h in range(GROUP)]
+        halves.append(jnp.concatenate(heads, axis=1))
+    out_ref[...] = jnp.concatenate(halves, axis=0).astype(jnp.bfloat16)
 
 
 def combine(parts):
     return pl.pallas_call(
         combine_kernel,
-        out_shape=jax.ShapeDtypeStruct((CH, HEADS * HD), jnp.bfloat16),
+        out_shape=jax.ShapeDtypeStruct((ROWS, GROUP * HD), jnp.bfloat16),
         in_specs=[pl.BlockSpec(memory_space=pltpu.VMEM)],
         out_specs=pl.BlockSpec(memory_space=pltpu.VMEM),
         cost_estimate=pl.CostEstimate(flops=10**8, bytes_accessed=12 * 10**5, transcendentals=0),
@@ -181,9 +185,11 @@
     )(parts)
 
 
-def project_kernel(place_ref, x_ref, y_ref, w_ref, v_ref, *outs):
+def project_kernel(place_ref, x0_ref, x1_ref, y0_ref, y1_ref, w_ref, v_ref, *outs):
     step = pl.program_id(0)
-    got = dot(x_ref[...], w_ref[...], ((1,), (0,))) + dot(y_ref[...], v_ref[...], ((1,), (0,)))
+    x = jnp.concatenate([x0_ref[...], x1_ref[...]], axis=1)
+    y = jnp.concatenate([y0_ref[...], y1_ref[...]], axis=1)
+    got = dot(x, w_ref[...], ((1,), (0,))) + dot(y, v_ref[...], ((1,), (0,)))
     got = got.astype(jnp.bfloat16)
     for n, out in enumerate(outs):
 
@@ -202,7 +208,7 @@
         to = lax.rem(place_ref[0] + hop, ZHI)
         return (0, (2 * to + place_ref[1]) * cuts + lax.rem(i, cuts))
 
-    rows, depth = x.shape
+    rows, depth = x[0].shape[0], 2 * x[0].shape[1]
     count = cuts * len(hops)
     return pl.pallas_call(
         project_kernel,
@@ -211,8 +217,7 @@
             num_scalar_prefetch=1,
             grid=(count,),
             in_specs=[
-                pl.BlockSpec((rows, depth), lambda i, p: (0, 0)),
-                pl.BlockSpec((rows, depth), lambda i, p: (0, 0)),
+                *[pl.BlockSpec((rows, depth // 2), lambda i, p: (0, 0)) for _ in range(4)],
                 pl.BlockSpec((depth, width), block),
                 pl.BlockSpec((depth, width), block),
             ],
@@ -225,7 +230,7 @@
             transcendentals=0,
         ),
         name="project",
-    )(place, x, y, w_own, w_other)
+    )(place, *x, *y, w_own, w_other)
 
 
 def added(*terms):
@@ -243,8 +248,6 @@
     z, core = t // 2, t % 2
     place = jnp.stack([z, core]).astype(jnp.int32)
 
-    q_many = jnp.broadcast_to(queries[None], (OUTER,) + queries.shape)
-    q_all = lax.all_to_all(q_many, "outer", 0, 0, tiled=True)
     early = stretch_order.reshape(OUTER, INNER, 2)[:, :, 0]
     j = lax.dynamic_index_in_dim(early, i, 1, keepdims=False)
     k_row = lax.dynamic_index_in_dim(early, o, 0, keepdims=False)
@@ -257,37 +260,37 @@
     )
 
     kv_own = jnp.concatenate([keys, values], axis=0)
-    kv_own = jnp.concatenate([kv_own, xor_to("inner", INNER, FAR, kv_own)], axis=0)
+    kv_far = xor_to("inner", INNER, FAR, kv_own)
+    q_many = jnp.broadcast_to(queries[None], (OUTER,) + queries.shape)
+    q_all = lax.all_to_all(q_many, "outer", 0, 0, tiled=True)
+    kv_own = jnp.concatenate([kv_own, kv_far], axis=0)
     kv_own, late, late_rows, place = lax.optimization_barrier((kv_own, late, late_rows, place))
     kv = [kv_own] + [xor_to("inner", INNER, s, kv_own) for s in range(1, FAR)]
 
     q_all, kv, w_send = lax.optimization_barrier((q_all, kv, w_out))
     w_other = xor_to("tensor", 2 * ZHI, 1, w_send)
 
-    part_e, part_l = partial_attention(o.reshape(1), late.reshape(-1), q_all, kv, late_rows)
-    part_e = lax.all_to_all(part_e, "outer", 0, 0, tiled=True)
-    part_e, part_l = lax.optimization_barrier((part_e, part_l))
-    part_l = lax.all_to_all(part_l, "outer", 0, 0, tiled=True)
+    own, sel = o.reshape(1), late.reshape(-1)
+    parts = []
+    for g in range(HEADS // GROUP):
+        part = partial_attention(own, sel, q_all, kv, late_rows, g)
+        parts.append(lax.all_to_all(part, "outer", 0, 0, tiled=True))
+    x, y = [], []
+    for g in range(HEADS // GROUP):
+        x.append(combine(parts[g]))
+        y.append(xor_to("tensor", 2 * ZHI, 1, x[-1]))
 
     up = [(n, (n + 2) % (2 * ZHI)) for n in range(2 * ZHI)]
     down = [(n, (n - 2) % (2 * ZHI)) for n in range(2 * ZHI)]
-    results = []
-    for half in range(2):
-        x = combine(part_l if half else part_e)
-        y = xor_to("tensor", 2 * ZHI, 1, x)
-        far_a, far_b = project(place, x, y, w_out, w_other, (2,), HALF)
-        relay_a = lax.ppermute(far_a, "tensor", up)
-        relay_b = lax.ppermute(far_b, "tensor", down)
-        to_up, to_down, mine = project(place, x, y, w_out, w_other, (1, 3, 0), 2 * HALF)
-        zero = jnp.zeros((), jnp.bfloat16)
-        to_up = added(to_up, lax.pad(relay_a, zero, ((0, 0, 0), (0, HALF, 0))))
-        to_down = added(to_down, lax.pad(relay_b, zero, ((0, 0, 0), (HALF, 0, 0))))
-        if half == 0:
-            part_l, to_up, to_down = lax.optimization_barrier((part_l, to_up, to_down))
-        below = lax.ppermute(to_up, "tensor", up)
-        above = lax.ppermute(to_down, "tensor", down)
-        results.append(added(mine, below, above))
-    return jnp.concatenate(results, axis=0)
+    far_a, far_b = project(place, x, y, w_out, w_other, (2,), HALF)
+    relay_a = lax.ppermute(far_a, "tensor", up)
+    relay_b = lax.ppermute(far_b, "tensor", down)
+    up_a, up_b, down_a, down_b, own_a, own_b = project(place, x, y, w_out, w_other, (1, 3, 0), HALF)
+    plain_b = lax.ppermute(up_b, "tensor", up)
+    plain_a = lax.ppermute(down_a, "tensor", down)
+    sum_a = lax.ppermute(added(up_a, relay_a), "tensor", up)
+    sum_b = lax.ppermute(added(down_b, relay_b), "tensor", down)
+    return jnp.concatenate([added(own_a, plain_a, sum_a), added(own_b, plain_b, sum_b)], axis=1)
 
 
 def solution(mesh):

time: 230 us -> 221 us (0.961)
  the two profiles are of different devices: /device:TPU:103 before, /device:TPU:7 now
where the time goes in v1:
time: 221 us; the launch traced here: 219 us
  starting transfers between devices  100 us (45%)
  waiting for transfers between devices  70.7 us (32%)
  Pallas kernels  36.4 us (16%)
  local copies, waits for them, and re-layouts  6.36 us (3%)
  other arithmetic  5.46 us (2%)
    ppermute x7, starting transfers between devices, xor_to(): return lax.ppermute(x, axis, [(n, n ^ mask) for n in range(size)])  35.5 us
    ppermute x1, waiting for transfers between devices, shards(): relay_b = lax.ppermute(far_b, 'tensor', down)  30.1 us
    pallas_call x2, Pallas kernels, partial_attention(): pl.pallas_call(attention_kernel, out_shape=jax.ShapeDtypeStruct((OUTER, H...  21.8 us
    ppermute x1, waiting for transfers between devices, shards(): sum_b = lax.ppermute(added(down_b, relay_b), 'tensor', down)  15.9 us
    all_to_all x2, waiting for transfers between devices, shards(): parts.append(lax.all_to_all(part, 'outer', 0, 0, tiled=True))  14.9 us
    ppermute x1, starting transfers between devices, shards(): relay_a = lax.ppermute(far_a, 'tensor', up)  13.9 us
    all_to_all x2, starting transfers between devices, shards(): parts.append(lax.all_to_all(part, 'outer', 0, 0, tiled=True))  12.3 us
    ppermute x1, starting transfers between devices, shards(): plain_a = lax.ppermute(down_a, 'tensor', down)  12.1 us
  transfers between devices with their start and end apart: 16, of which 8 were waited for; matrix products, arithmetic and copies ran while one was open for 3% of the time, Pallas kernels for 15%

profile of v1, /device:TPU:7, one launch (start us, length us, event | category | flops | bytes accessed | tf_op | source)
XLA Modules:
  0.0 219.4 jit_solution(14066119089745793581)
XLA Ops:
  0.0 2.4 %broadcast_in_dim.39 = bf16[16,128,512]{2,1,0:T(8,128)(2,1)} broadcast(bf16[128,512]{1,0:T(8,128)(2,1)} %param.5), dimensions={1,2} | broadcast | bytes 2228224 | tf_op jit(solution)/shard_map/broadcast_in_dim | solution.py:264
  2.4 7.0 %all-to-all-start = ((bf16[16,128,512]{2,1,0:T(8,128)(2,1)}), bf16[16,128,512]{2,1,0:T(8,128)(2,1)S(1)}, u32[]{:S(2)}, u32[]{:S(2)}) async-start(bf16[16,128,512]{2,1,0:T(8,128)(2,1)} %broadcast_in_dim.39), calls=%async_computation | async-start | bytes 4194304 | tf_op jit(solution)/shard_map/all_to_all | solution.py:265
  9.5 8.8 %collective-permute-start = (bf16[256,128]{1,0:T(8,128)(2,1)S(1)}, bf16[256,128]{1,0:T(8,128)(2,1)S(1)}, u32[]{:S(2)}, u32[]{:S(2)}) collective-permute-start(bf16[256,128]{1,0:T(8,128)(2,1)S(1)} %pad_maximum_fusion.2), channel_id=1, source_target_pairs={{0,32},{8,40},{16,48},{24,56},{32,0},{40,8},{48,16},{56,24},{1,33}... | collective-permute-start | bytes 196616 | tf_op jit(solution)/shard_map/ppermute | solution.py:241
  20.9 8.9 %collective-permute-start.3 = (bf16[512,128]{1,0:T(8,128)(2,1)S(1)}, bf16[512,128]{1,0:T(8,128)(2,1)S(1)}, u32[]{:S(2)}, u32[]{:S(2)}) collective-permute-start(bf16[512,128]{1,0:T(8,128)(2,1)S(1)} %pad_maximum_fusion.1.refs_0_), channel_id=1, source_target_pairs={{0,24},{8,16},{16,8},{24,0},{32,56},{40,48},{48,40},{56,32},{1,25}... | collective-permute-start | bytes 393224 | tf_op jit(solution)/shard_map/ppermute | solution.py:241
  29.8 1.9 collective-permute-start.2
  31.7 2.2 collective-permute-start.1
  34.0 2.8 %collective-permute-done.2.refs_2_ = bf16[512,128]{1,0:T(8,128)(2,1)S(1)} collective-permute-done((bf16[512,128]{1,0:T(8,128)(2,1)S(1)}, bf16[512,128]{1,0:T(8,128)(2,1)S(1)}, u32[]{:S(2)}, u32[]{:S(2)}) %collective-permute-start.2) | collective-permute-done | bytes 131104 | tf_op jit(solution)/shard_map/ppermute | solution.py:241
  36.7 3.7 %collective-permute-done.1.refs_1_ = bf16[512,128]{1,0:T(8,128)(2,1)S(1)} collective-permute-done((bf16[512,128]{1,0:T(8,128)(2,1)S(1)}, bf16[512,128]{1,0:T(8,128)(2,1)S(1)}, u32[]{:S(2)}, u32[]{:S(2)}) %collective-permute-start.1) | collective-permute-done | bytes 131104 | tf_op jit(solution)/shard_map/ppermute | solution.py:241
  40.4 5.4 %collective-permute-start.6 = (bf16[512,8192]{1,0:T(8,128)(2,1)}, bf16[512,8192]{1,0:T(8,128)(2,1)}, u32[]{:S(2)}, u32[]{:S(2)}) collective-permute-start(bf16[512,8192]{1,0:T(8,128)(2,1)} %w_ref.3), channel_id=1, source_target_pairs={{0,1},{1,0},{2,3},{3,2},{4,5},{5,4},{6,7},{7,6},{8,9},{9,8},{10,11... | collective-permute-start | bytes 25165832 | tf_op jit(solution)/shard_map/ppermute | solution.py:241
  46.4 10.9 %partial_attention.3 = bf16[16,144,256]{2,1,0:T(8,128)(2,1)} custom-call(s32[1]{0:T(128)} %bitcast.2.own_ref, s32[128]{0:T(128)} %reshape.29.sel_ref, bf16[16,128,512]{2,1,0:T(8,128)(2,1)} %copy-done.2, bf16[512,128]{1,0:T(8,128)(2,1)} %copy-done.3, bf16[512,128]{1,0:T(8,128)(2,1)} %copy-done.11, bf16[512,128]{1,0:T(8,128)(2,1)} %copy-done.10, ...), custom_call_target="tpu_custom_call" | custom-call | flops 4000000000 | bytes 3000000 | tf_op jit(solution)/shard_map/partial_attention/pallas_call | solution.py:130
  57.3 6.6 %all-to-all-start.2 = ((bf16[16,144,256]{2,1,0:T(8,128)(2,1)}), bf16[16,144,256]{2,1,0:T(8,128)(2,1)S(1)}, u32[]{:S(2)}, u32[]{:S(2)}) async-start(bf16[16,144,256]{2,1,0:T(8,128)(2,1)} %partial_attention.3), calls=%async_computation.2 | async-start | bytes 2359296 | tf_op jit(solution)/shard_map/all_to_all | solution.py:277
  63.9 10.9 %partial_attention.2 = bf16[16,144,256]{2,1,0:T(8,128)(2,1)} custom-call(s32[1]{0:T(128)} %bitcast.2.own_ref, s32[128]{0:T(128)} %reshape.29.sel_ref, bf16[16,128,512]{2,1,0:T(8,128)(2,1)} %copy-done.2, bf16[512,128]{1,0:T(8,128)(2,1)} %copy-done.3, bf16[512,128]{1,0:T(8,128)(2,1)} %copy-done.11, bf16[512,128]{1,0:T(8,128)(2,1)} %copy-done.10, ...), custom_call_target="tpu_custom_call" | custom-call | flops 4000000000 | bytes 3000000 | tf_op jit(solution)/shard_map/partial_attention/pallas_call | solution.py:130
  74.8 5.7 %all-to-all-done.2.part_ref = bf16[16,144,256]{2,1,0:T(8,128)(2,1)S(1)} async-done(((bf16[16,144,256]{2,1,0:T(8,128)(2,1)}), bf16[16,144,256]{2,1,0:T(8,128)(2,1)S(1)}, u32[]{:S(2)}, u32[]{:S(2)}) %all-to-all-start.2) | async-done | bytes 1179680 | tf_op jit(solution)/shard_map/all_to_all | solution.py:277
  80.5 5.7 %all-to-all-start.1 = ((bf16[16,144,256]{2,1,0:T(8,128)(2,1)}), bf16[16,144,256]{2,1,0:T(8,128)(2,1)S(1)}, u32[]{:S(2)}, u32[]{:S(2)}) async-start(bf16[16,144,256]{2,1,0:T(8,128)(2,1)} %partial_attention.2), calls=%async_computation.1 | async-start | bytes 2359296 | tf_op jit(solution)/shard_map/all_to_all | solution.py:277
  86.2 2.2 %combine.3.x1_ref = bf16[128,256]{1,0:T(8,128)(2,1)} custom-call(bf16[16,144,256]{2,1,0:T(8,128)(2,1)} %copy-done), custom_call_target="tpu_custom_call" | custom-call | flops 100000000 | bytes 1200000 | tf_op jit(solution)/shard_map/combine/pallas_call | solution.py:178
  88.4 3.9 %collective-permute-start.5 = (bf16[128,256]{1,0:T(8,128)(2,1)}, bf16[128,256]{1,0:T(8,128)(2,1)S(1)}, u32[]{:S(2)}, u32[]{:S(2)}) collective-permute-start(bf16[128,256]{1,0:T(8,128)(2,1)} %combine.3.x1_ref), channel_id=1, source_target_pairs={{0,1},{1,0},{2,3},{3,2},{4,5},{5,4},{6,7},{7,6},{8,9},{9,8},{10,11... | collective-permute-start | bytes 196616 | tf_op jit(solution)/shard_map/ppermute | solution.py:241
  92.3 9.3 %all-to-all-done.1.part_ref = bf16[16,144,256]{2,1,0:T(8,128)(2,1)S(1)} async-done(((bf16[16,144,256]{2,1,0:T(8,128)(2,1)}), bf16[16,144,256]{2,1,0:T(8,128)(2,1)S(1)}, u32[]{:S(2)}, u32[]{:S(2)}) %all-to-all-start.1) | async-done | bytes 1179680 | tf_op jit(solution)/shard_map/all_to_all | solution.py:277
  101.6 1.1 copy-done.1
  102.7 2.2 %combine.2.x0_ref = bf16[128,256]{1,0:T(8,128)(2,1)} custom-call(bf16[16,144,256]{2,1,0:T(8,128)(2,1)} %copy-done.1), custom_call_target="tpu_custom_call" | custom-call | flops 100000000 | bytes 1200000 | tf_op jit(solution)/shard_map/combine/pallas_call | solution.py:178
  104.9 4.4 %collective-permute-start.4 = (bf16[128,256]{1,0:T(8,128)(2,1)}, bf16[128,256]{1,0:T(8,128)(2,1)S(1)}, u32[]{:S(2)}, u32[]{:S(2)}) collective-permute-start(bf16[128,256]{1,0:T(8,128)(2,1)} %combine.2.x0_ref), channel_id=1, source_target_pairs={{0,1},{1,0},{2,3},{3,2},{4,5},{5,4},{6,7},{7,6},{8,9},{9,8},{10,11... | collective-permute-start | bytes 196616 | tf_op jit(solution)/shard_map/ppermute | solution.py:241
  109.3 1.1 collective-permute-done.4.y0_ref
  111.0 3.3 %project.3 = (bf16[128,512]{1,0:T(8,128)(2,1)}, bf16[128,512]{1,0:T(8,128)(2,1)}) custom-call(s32[2]{0:T(128)} %pad_add_fusion.place_ref, bf16[128,256]{1,0:T(8,128)(2,1)} %combine.2.x0_ref, bf16[128,256]{1,0:T(8,128)(2,1)} %combine.3.x1_ref, bf16[128,256]{1,0:T(8,128)(2,1)} %copy-done.7, bf16[128,256]{1,0:T(8,128)(2,1)} %copy-done.6, ...), custom_call_target="tpu_custom_call" | custom-call | flops 2684354560 | bytes 2097152 | tf_op jit(solution)/shard_map/project/pallas_call | solution.py:213
  114.3 13.9 %collective-permute-start.8 = (bf16[128,512]{1,0:T(8,128)(2,1)}, bf16[128,512]{1,0:T(8,128)(2,1)S(1)}, u32[]{:S(2)}, u32[]{:S(2)}) collective-permute-start(bf16[128,512]{1,0:T(8,128)(2,1)} %get-tuple-element.36), channel_id=1, source_target_pairs={{0,2},{1,3},{2,4},{3,5},{4,6},{5,7},{6,0},{7,1},{8,10},{9,11},{10,... | collective-permute-start | bytes 393224 | tf_op jit(solution)/shard_map/ppermute | solution.py:286
  128.2 7.2 %collective-permute-start.11 = (bf16[128,512]{1,0:T(8,128)(2,1)}, bf16[128,512]{1,0:T(8,128)(2,1)S(1)}, u32[]{:S(2)}, u32[]{:S(2)}) collective-permute-start(bf16[128,512]{1,0:T(8,128)(2,1)} %get-tuple-element.40), channel_id=1, source_target_pairs={{0,6},{1,7},{2,0},{3,1},{4,2},{5,3},{6,4},{7,5},{8,14},{9,15},{10,... | collective-permute-start | bytes 393224 | tf_op jit(solution)/shard_map/ppermute | solution.py:287
  135.4 6.9 %project.2 = (bf16[128,512]{1,0:T(8,128)(2,1)}, bf16[128,512]{1,0:T(8,128)(2,1)}, bf16[128,512]{1,0:T(8,128)(2,1)}, bf16[128,512]{1,0:T(8,128)(2,1)}, bf16[128,5...) custom-call(s32[2]{0:T(128)} %pad_add_fusion.place_ref, bf16[128,256]{1,0:T(8,128)(2,1)} %combine.2.x0_ref, ...), custom_call_target="tpu_custom_call" | custom-call | flops 8053063680 | bytes 6291456 | tf_op jit(solution)/shard_map/project/pallas_call | solution.py:213
  142.4 12.1 %collective-permute-start.7 = (bf16[128,512]{1,0:T(8,128)(2,1)}, bf16[128,512]{1,0:T(8,128)(2,1)S(1)}, u32[]{:S(2)}, u32[]{:S(2)}) collective-permute-start(bf16[128,512]{1,0:T(8,128)(2,1)} %get-tuple-element.34), channel_id=1, source_target_pairs={{0,6},{1,7},{2,0},{3,1},{4,2},{5,3},{6,4},{7,5},{8,14},{9,15},{10,... | collective-permute-start | bytes 393224 | tf_op jit(solution)/shard_map/ppermute | solution.py:290
  154.5 1.9 collective-permute-start.10
  157.3 8.3 %collective-permute-start.9 = (bf16[128,512]{1,0:T(8,128)(2,1)S(1)}, bf16[128,512]{1,0:T(8,128)(2,1)S(1)}, u32[]{:S(2)}, u32[]{:S(2)}) collective-permute-start(bf16[128,512]{1,0:T(8,128)(2,1)S(1)} %add_convert_fusion.3), channel_id=1, source_target_pairs={{0,2},{1,3},{2,4},{3,5},{4,6},{5,7},{6,0},{7,1},{8,10},{9,11},{10,... | collective-permute-start | bytes 393224 | tf_op jit(solution)/shard_map/ppermute | solution.py:291
  165.6 30.1 %collective-permute-done.11 = bf16[128,512]{1,0:T(8,128)(2,1)S(1)} collective-permute-done((bf16[128,512]{1,0:T(8,128)(2,1)}, bf16[128,512]{1,0:T(8,128)(2,1)S(1)}, u32[]{:S(2)}, u32[]{:S(2)}) %collective-permute-start.11) | collective-permute-done | bytes 131104 | tf_op jit(solution)/shard_map/ppermute | solution.py:287
  196.6 1.9 collective-permute-start.12
  198.6 2.3 %collective-permute-done.7 = bf16[128,512]{1,0:T(8,128)(2,1)S(1)} collective-permute-done((bf16[128,512]{1,0:T(8,128)(2,1)}, bf16[128,512]{1,0:T(8,128)(2,1)S(1)}, u32[]{:S(2)}, u32[]{:S(2)}) %collective-permute-start.7) | collective-permute-done | bytes 131104 | tf_op jit(solution)/shard_map/ppermute | solution.py:290
  201.9 15.9 %collective-permute-done.12 = bf16[128,512]{1,0:T(8,128)(2,1)S(1)} collective-permute-done((bf16[128,512]{1,0:T(8,128)(2,1)S(1)}, bf16[128,512]{1,0:T(8,128)(2,1)S(1)}, u32[]{:S(2)}, u32[]{:S(2)}) %collective-permute-start.12) | collective-permute-done | bytes 131104 | tf_op jit(solution)/shard_map/ppermute | solution.py:292
  (49 shorter events, 8.3 us)
Async XLA Ops:
  2.4 7.0 %copy-start.4 = (bf16[128,128]{1,0:T(8,128)(2,1)S(1)}, bf16[128,128]{1,0:T(8,128)(2,1)}, u32[]{:S(2)}) copy-start(bf16[128,128]{1,0:T(8,128)(2,1)} %param.7) | copy-start | bytes 98308
  2.4 7.0 %copy-start.5 = (bf16[128,128]{1,0:T(8,128)(2,1)S(1)}, bf16[128,128]{1,0:T(8,128)(2,1)}, u32[]{:S(2)}) copy-start(bf16[128,128]{1,0:T(8,128)(2,1)} %param.6) | copy-start | bytes 98308
  2.4 15.9 %copy-start.8 = (s32[256]{0:T(256)S(1)}, s32[256]{0:T(256)}, u32[]{:S(2)}) copy-start(s32[256]{0:T(256)} %param.8) | copy-start | bytes 3076
  2.4 37.9 %all-to-all-start = ((bf16[16,128,512]{2,1,0:T(8,128)(2,1)}), bf16[16,128,512]{2,1,0:T(8,128)(2,1)S(1)}, u32[]{:S(2)}, u32[]{:S(2)}) async-start(bf16[16,128,512]{2,1,0:T(8,128)(2,1)} %broadcast_in_dim.39), calls=%async_computation | async-start | bytes 4194304 | tf_op jit(solution)/shard_map/all_to_all | solution.py:265
  9.5 10.6 %collective-permute-start = (bf16[256,128]{1,0:T(8,128)(2,1)S(1)}, bf16[256,128]{1,0:T(8,128)(2,1)S(1)}, u32[]{:S(2)}, u32[]{:S(2)}) collective-permute-start(bf16[256,128]{1,0:T(8,128)(2,1)S(1)} %pad_maximum_fusion.2), channel_id=1, source_target_pairs={{0,32},{8,40},{16,48},{24,56},{32,0},{40,8},{48,16},{56,24},{1,33}... | collective-permute-start | bytes 196616 | tf_op jit(solution)/shard_map/ppermute | solution.py:241
  20.1 26.2 %copy-start.3 = (bf16[512,128]{1,0:T(8,128)(2,1)}, bf16[512,128]{1,0:T(8,128)(2,1)S(1)}, u32[]{:S(2)}) copy-start(bf16[512,128]{1,0:T(8,128)(2,1)S(1)} %pad_maximum_fusion.1.refs_0_) | copy-start | bytes 393220
  20.9 13.1 %collective-permute-start.3 = (bf16[512,128]{1,0:T(8,128)(2,1)S(1)}, bf16[512,128]{1,0:T(8,128)(2,1)S(1)}, u32[]{:S(2)}, u32[]{:S(2)}) collective-permute-start(bf16[512,128]{1,0:T(8,128)(2,1)S(1)} %pad_maximum_fusion.1.refs_0_), channel_id=1, source_target_pairs={{0,24},{8,16},{16,8},{24,0},{32,56},{40,48},{48,40},{56,32},{1,25}... | collective-permute-start | bytes 393224 | tf_op jit(solution)/shard_map/ppermute | solution.py:241
  29.8 6.9 %collective-permute-start.2 = (bf16[512,128]{1,0:T(8,128)(2,1)S(1)}, bf16[512,128]{1,0:T(8,128)(2,1)S(1)}, u32[]{:S(2)}, u32[]{:S(2)}) collective-permute-start(bf16[512,128]{1,0:T(8,128)(2,1)S(1)} %pad_maximum_fusion.1.refs_0_), channel_id=1, source_target_pairs={{0,16},{8,24},{16,0},{24,8},{32,48},{40,56},{48,32},{56,40},{1,17}... | collective-permute-start | bytes 393224 | tf_op jit(solution)/shard_map/ppermute | solution.py:241
  31.7 8.6 %collective-permute-start.1 = (bf16[512,128]{1,0:T(8,128)(2,1)S(1)}, bf16[512,128]{1,0:T(8,128)(2,1)S(1)}, u32[]{:S(2)}, u32[]{:S(2)}) collective-permute-start(bf16[512,128]{1,0:T(8,128)(2,1)S(1)} %pad_maximum_fusion.1.refs_0_), channel_id=1, source_target_pairs={{0,8},{8,0},{16,24},{24,16},{32,40},{40,32},{48,56},{56,48},{1,9},... | collective-permute-start | bytes 393224 | tf_op jit(solution)/shard_map/ppermute | solution.py:241
  33.9 12.4 %copy-start.9 = (bf16[512,128]{1,0:T(8,128)(2,1)}, bf16[512,128]{1,0:T(8,128)(2,1)S(1)}, u32[]{:S(2)}) copy-start(bf16[512,128]{1,0:T(8,128)(2,1)S(1)} %collective-permute-done.3.refs_3_) | copy-start | bytes 393220
  36.7 9.7 %copy-start.10 = (bf16[512,128]{1,0:T(8,128)(2,1)}, bf16[512,128]{1,0:T(8,128)(2,1)S(1)}, u32[]{:S(2)}) copy-start(bf16[512,128]{1,0:T(8,128)(2,1)S(1)} %collective-permute-done.2.refs_2_) | copy-start | bytes 393220
  40.4 6.0 %copy-start.11 = (bf16[512,128]{1,0:T(8,128)(2,1)}, bf16[512,128]{1,0:T(8,128)(2,1)S(1)}, u32[]{:S(2)}) copy-start(bf16[512,128]{1,0:T(8,128)(2,1)S(1)} %collective-permute-done.1.refs_1_) | copy-start | bytes 393220
  40.4 6.0 %copy-start.2 = (bf16[16,128,512]{2,1,0:T(8,128)(2,1)}, bf16[16,128,512]{2,1,0:T(8,128)(2,1)S(1)}, u32[]{:S(2)}) copy-start(bf16[16,128,512]{2,1,0:T(8,128)(2,1)S(1)} %all-to-all-done.q_ref) | copy-start | bytes 6291460
  40.4 70.0 %collective-permute-start.6 = (bf16[512,8192]{1,0:T(8,128)(2,1)}, bf16[512,8192]{1,0:T(8,128)(2,1)}, u32[]{:S(2)}, u32[]{:S(2)}) collective-permute-start(bf16[512,8192]{1,0:T(8,128)(2,1)} %w_ref.3), channel_id=1, source_target_pairs={{0,1},{1,0},{2,3},{3,2},{4,5},{5,4},{6,7},{7,6},{8,9},{9,8},{10,11... | collective-permute-start | bytes 25165832 | tf_op jit(solution)/shard_map/ppermute | solution.py:241
  57.3 23.2 %all-to-all-start.2 = ((bf16[16,144,256]{2,1,0:T(8,128)(2,1)}), bf16[16,144,256]{2,1,0:T(8,128)(2,1)S(1)}, u32[]{:S(2)}, u32[]{:S(2)}) async-start(bf16[16,144,256]{2,1,0:T(8,128)(2,1)} %partial_attention.3), calls=%async_computation.2 | async-start | bytes 2359296 | tf_op jit(solution)/shard_map/all_to_all | solution.py:277
  80.4 5.7 %copy-start = (bf16[16,144,256]{2,1,0:T(8,128)(2,1)}, bf16[16,144,256]{2,1,0:T(8,128)(2,1)S(1)}, u32[]{:S(2)}) copy-start(bf16[16,144,256]{2,1,0:T(8,128)(2,1)S(1)} %all-to-all-done.2.part_ref) | copy-start | bytes 3538948
  80.5 21.1 %all-to-all-start.1 = ((bf16[16,144,256]{2,1,0:T(8,128)(2,1)}), bf16[16,144,256]{2,1,0:T(8,128)(2,1)S(1)}, u32[]{:S(2)}, u32[]{:S(2)}) async-start(bf16[16,144,256]{2,1,0:T(8,128)(2,1)} %partial_attention.2), calls=%async_computation.1 | async-start | bytes 2359296 | tf_op jit(solution)/shard_map/all_to_all | solution.py:277
  88.4 20.9 %collective-permute-start.5 = (bf16[128,256]{1,0:T(8,128)(2,1)}, bf16[128,256]{1,0:T(8,128)(2,1)S(1)}, u32[]{:S(2)}, u32[]{:S(2)}) collective-permute-start(bf16[128,256]{1,0:T(8,128)(2,1)} %combine.3.x1_ref), channel_id=1, source_target_pairs={{0,1},{1,0},{2,3},{3,2},{4,5},{5,4},{6,7},{7,6},{8,9},{9,8},{10,11... | collective-permute-start | bytes 196616 | tf_op jit(solution)/shard_map/ppermute | solution.py:241
  101.6 1.1 copy-start.1
  104.9 5.5 %collective-permute-start.4 = (bf16[128,256]{1,0:T(8,128)(2,1)}, bf16[128,256]{1,0:T(8,128)(2,1)S(1)}, u32[]{:S(2)}, u32[]{:S(2)}) collective-permute-start(bf16[128,256]{1,0:T(8,128)(2,1)} %combine.2.x0_ref), channel_id=1, source_target_pairs={{0,1},{1,0},{2,3},{3,2},{4,5},{5,4},{6,7},{7,6},{8,9},{9,8},{10,11... | collective-permute-start | bytes 196616 | tf_op jit(solution)/shard_map/ppermute | solution.py:241
  109.3 1.1 copy-start.6
  110.4 0.6 copy-start.7
  114.3 42.1 %collective-permute-start.8 = (bf16[128,512]{1,0:T(8,128)(2,1)}, bf16[128,512]{1,0:T(8,128)(2,1)S(1)}, u32[]{:S(2)}, u32[]{:S(2)}) collective-permute-start(bf16[128,512]{1,0:T(8,128)(2,1)} %get-tuple-element.36), channel_id=1, source_target_pairs={{0,2},{1,3},{2,4},{3,5},{4,6},{5,7},{6,0},{7,1},{8,10},{9,11},{10,... | collective-permute-start | bytes 393224 | tf_op jit(solution)/shard_map/ppermute | solution.py:286
  128.2 67.5 %collective-permute-start.11 = (bf16[128,512]{1,0:T(8,128)(2,1)}, bf16[128,512]{1,0:T(8,128)(2,1)S(1)}, u32[]{:S(2)}, u32[]{:S(2)}) collective-permute-start(bf16[128,512]{1,0:T(8,128)(2,1)} %get-tuple-element.40), channel_id=1, source_target_pairs={{0,6},{1,7},{2,0},{3,1},{4,2},{5,3},{6,4},{7,5},{8,14},{9,15},{10,... | collective-permute-start | bytes 393224 | tf_op jit(solution)/shard_map/ppermute | solution.py:287
  142.4 58.5 %collective-permute-start.7 = (bf16[128,512]{1,0:T(8,128)(2,1)}, bf16[128,512]{1,0:T(8,128)(2,1)S(1)}, u32[]{:S(2)}, u32[]{:S(2)}) collective-permute-start(bf16[128,512]{1,0:T(8,128)(2,1)} %get-tuple-element.34), channel_id=1, source_target_pairs={{0,6},{1,7},{2,0},{3,1},{4,2},{5,3},{6,4},{7,5},{8,14},{9,15},{10,... | collective-permute-start | bytes 393224 | tf_op jit(solution)/shard_map/ppermute | solution.py:290
  154.5 47.4 %collective-permute-start.10 = (bf16[128,512]{1,0:T(8,128)(2,1)}, bf16[128,512]{1,0:T(8,128)(2,1)S(1)}, u32[]{:S(2)}, u32[]{:S(2)}) collective-permute-start(bf16[128,512]{1,0:T(8,128)(2,1)} %get-tuple-element.38), channel_id=1, source_target_pairs={{0,2},{1,3},{2,4},{3,5},{4,6},{5,7},{6,0},{7,1},{8,10},{9,11},{10,... | collective-permute-start | bytes 393224 | tf_op jit(solution)/shard_map/ppermute | solution.py:289
  157.3 43.5 %collective-permute-start.9 = (bf16[128,512]{1,0:T(8,128)(2,1)S(1)}, bf16[128,512]{1,0:T(8,128)(2,1)S(1)}, u32[]{:S(2)}, u32[]{:S(2)}) collective-permute-start(bf16[128,512]{1,0:T(8,128)(2,1)S(1)} %add_convert_fusion.3), channel_id=1, source_target_pairs={{0,2},{1,3},{2,4},{3,5},{4,6},{5,7},{6,0},{7,1},{8,10},{9,11},{10,... | collective-permute-start | bytes 393224 | tf_op jit(solution)/shard_map/ppermute | solution.py:291
  196.6 21.1 %collective-permute-start.12 = (bf16[128,512]{1,0:T(8,128)(2,1)S(1)}, bf16[128,512]{1,0:T(8,128)(2,1)S(1)}, u32[]{:S(2)}, u32[]{:S(2)}) collective-permute-start(bf16[128,512]{1,0:T(8,128)(2,1)S(1)} %add_convert_fusion.1), channel_id=1, source_target_pairs={{0,6},{1,7},{2,0},{3,1},{4,2},{5,3},{6,4},{7,5},{8,14},{9,15},{10,... | collective-permute-start | bytes 393224 | tf_op jit(solution)/shard_map/ppermute | solution.py:292

commit v2 on v1

--- a/solution.py
+++ b/solution.py
@@ -9,20 +9,19 @@
 
 
 HD = 128
-HEADS = 4
 CH = 64
 ROWS = 2 * CH
 OUTER = 16
 INNER = 8
 FAR = 4
 ZHI = 4
-GROUP = 2
+GROUP = 4
 QC = GROUP * CH
 EXTRA = 16
 NEG = -1e30
 COEF = math.log2(math.e) / math.sqrt(HD)
 PER = 4
-HALF = 512
+OUT = 1024
 
 
 def dot(a, b, dims):
@@ -147,7 +146,7 @@
             pltpu.VMEM((HD, n_keys), jnp.bfloat16),
         ],
         compiler_params=pltpu.CompilerParams(dimension_semantics=("arbitrary",)),
-        cost_estimate=pl.CostEstimate(flops=4 * 10**9, bytes_accessed=3 * 10**6, transcendentals=2 * 10**6),
+        cost_estimate=pl.CostEstimate(flops=8 * 10**9, bytes_accessed=6 * 10**6, transcendentals=4 * 10**6),
         name="partial_attention",
     )(own, sel, q_all, *kv, late)
 
@@ -185,52 +184,49 @@
     )(parts)
 
 
-def project_kernel(place_ref, x0_ref, x1_ref, y0_ref, y1_ref, w_ref, v_ref, *outs):
+def project_kernel(place_ref, x_ref, y_ref, w_ref, v_ref, *outs):
     step = pl.program_id(0)
-    x = jnp.concatenate([x0_ref[...], x1_ref[...]], axis=1)
-    y = jnp.concatenate([y0_ref[...], y1_ref[...]], axis=1)
-    got = dot(x, w_ref[...], ((1,), (0,))) + dot(y, v_ref[...], ((1,), (0,)))
+    got = dot(x_ref[...], w_ref[...], ((1,), (0,))) + dot(y_ref[...], v_ref[...], ((1,), (0,)))
     got = got.astype(jnp.bfloat16)
-    for n, out in enumerate(outs):
+    cuts = outs[0].shape[1] // got.shape[1]
+    for n in range(cuts * len(outs)):
+        at = (n % cuts) * got.shape[1]
 
         @pl.when(step == n)
         def _():
-            out[...] = got
-
-
-def project(place, x, y, w_own, w_other, hops, width):
-    cuts = 2 * HALF // width
+            outs[n // cuts][:, at : at + got.shape[1]] = got
+
+
+def project(blocks, x, y, w_own, w_other, width):
+    cuts = OUT // width
+    rows, depth = x.shape
+    count = blocks.shape[0]
 
     def block(i, place_ref):
-        hop = jnp.int32(hops[-1])
-        for n in range(len(hops) - 1):
-            hop = jnp.where(i // cuts == n, jnp.int32(hops[n]), hop)
-        to = lax.rem(place_ref[0] + hop, ZHI)
-        return (0, (2 * to + place_ref[1]) * cuts + lax.rem(i, cuts))
-
-    rows, depth = x[0].shape[0], 2 * x[0].shape[1]
-    count = cuts * len(hops)
+        return (0, place_ref[i // cuts] * cuts + lax.rem(i, cuts))
+
     return pl.pallas_call(
         project_kernel,
-        out_shape=[jax.ShapeDtypeStruct((rows, width), jnp.bfloat16)] * count,
+        out_shape=[jax.ShapeDtypeStruct((rows, OUT), jnp.bfloat16)] * count,
         grid_spec=pltpu.PrefetchScalarGridSpec(
             num_scalar_prefetch=1,
-            grid=(count,),
+            grid=(count * cuts,),
             in_specs=[
-                *[pl.BlockSpec((rows, depth // 2), lambda i, p: (0, 0)) for _ in range(4)],
+                pl.BlockSpec((rows, depth), lambda i, p: (0, 0)),
+                pl.BlockSpec((rows, depth), lambda i, p: (0, 0)),
                 pl.BlockSpec((depth, width), block),
                 pl.BlockSpec((depth, width), block),
             ],
-            out_specs=[pl.BlockSpec((rows, width), lambda i, p: (0, 0))] * count,
+            out_specs=[pl.BlockSpec((rows, OUT), lambda i, p: (0, 0))] * count,
         ),
         compiler_params=pltpu.CompilerParams(dimension_semantics=("arbitrary",)),
         cost_estimate=pl.CostEstimate(
-            flops=10 * 2 * rows * 2 * depth * width * count,
-            bytes_accessed=2 * depth * width * count * 2,
+            flops=10 * 2 * rows * 2 * depth * OUT * count,
+            bytes_accessed=2 * depth * OUT * count * 2,
             transcendentals=0,
         ),
         name="project",
-    )(place, *x, *y, w_own, w_other)
+    )(blocks, x, y, w_own, w_other)
 
 
 def added(*terms):
@@ -246,7 +242,9 @@
     i = lax.axis_index("inner")
     t = lax.axis_index("tensor")
     z, core = t // 2, t % 2
-    place = jnp.stack([z, core]).astype(jnp.int32)
+    ahead = 1 - 2 * core
+    hops = jnp.stack([2 + 0 * z, ZHI - ahead, ZHI + ahead, 0 * z]).astype(jnp.int32)
+    place = lax.rem(z + hops, ZHI) * 2 + core
 
     early = stretch_order.reshape(OUTER, INNER, 2)[:, :, 0]
     j = lax.dynamic_index_in_dim(early, i, 1, keepdims=False)
@@ -270,27 +268,21 @@
     q_all, kv, w_send = lax.optimization_barrier((q_all, kv, w_out))
     w_other = xor_to("tensor", 2 * ZHI, 1, w_send)
 
-    own, sel = o.reshape(1), late.reshape(-1)
-    parts = []
-    for g in range(HEADS // GROUP):
-        part = partial_attention(own, sel, q_all, kv, late_rows, g)
-        parts.append(lax.all_to_all(part, "outer", 0, 0, tiled=True))
-    x, y = [], []
-    for g in range(HEADS // GROUP):
-        x.append(combine(parts[g]))
-        y.append(xor_to("tensor", 2 * ZHI, 1, x[-1]))
-
-    up = [(n, (n + 2) % (2 * ZHI)) for n in range(2 * ZHI)]
-    down = [(n, (n - 2) % (2 * ZHI)) for n in range(2 * ZHI)]
-    far_a, far_b = project(place, x, y, w_out, w_other, (2,), HALF)
-    relay_a = lax.ppermute(far_a, "tensor", up)
-    relay_b = lax.ppermute(far_b, "tensor", down)
-    up_a, up_b, down_a, down_b, own_a, own_b = project(place, x, y, w_out, w_other, (1, 3, 0), HALF)
-    plain_b = lax.ppermute(up_b, "tensor", up)
-    plain_a = lax.ppermute(down_a, "tensor", down)
-    sum_a = lax.ppermute(added(up_a, relay_a), "tensor", up)
-    sum_b = lax.ppermute(added(down_b, relay_b), "tensor", down)
-    return jnp.concatenate([added(own_a, plain_a, sum_a), added(own_b, plain_b, sum_b)], axis=1)
+    part = partial_attention(o.reshape(1), late.reshape(-1), q_all, kv, late_rows, 0)
+    part = lax.all_to_all(part, "outer", 0, 0, tiled=True)
+    x = combine(part)
+    y = xor_to("tensor", 2 * ZHI, 1, x)
+
+    count = 2 * ZHI
+    ahead_of = [(n + 2 - 4 * (n % 2)) % count for n in range(count)]
+    along = [(n, ahead_of[n]) for n in range(count)]
+    against = [(ahead_of[n], n) for n in range(count)]
+    (far,) = project(place[:1], x, y, w_out, w_other, 512)
+    relay = lax.ppermute(far, "tensor", along)
+    behind, front, mine = project(place[1:], x, y, w_out, w_other, 512)
+    plain = lax.ppermute(behind, "tensor", against)
+    merged = lax.ppermute(added(front, relay), "tensor", along)
+    return added(mine, plain, merged)
 
 
 def solution(mesh):

time: 221 us -> 201 us (0.910)
  the two profiles are of different devices: /device:TPU:7 before, /device:TPU:97 now
where the time goes in v2:
time: 201 us
  starting transfers between devices  67.2 us (33%)
  waiting for transfers between devices  62.5 us (31%)
  blocking collectives  37.2 us (19%)
  Pallas kernels  24.5 us (12%)
  local copies, waits for them, and re-layouts  5.88 us (3%)
  other arithmetic  3.16 us (2%)
    ppermute x1, waiting for transfers between devices, shards(): relay = lax.ppermute(far, 'tensor', along)  50.6 us
    all_to_all x1, blocking collectives, shards(): part = lax.all_to_all(part, 'outer', 0, 0, tiled=True)  37.2 us
    ppermute x6, starting transfers between devices, xor_to(): return lax.ppermute(x, axis, [(n, n ^ mask) for n in range(size)])  26.8 us
    ppermute x1, starting transfers between devices, shards(): relay = lax.ppermute(far, 'tensor', along)  18.8 us
    ppermute x1, starting transfers between devices, shards(): merged = lax.ppermute(added(front, relay), 'tensor', along)  12.7 us
    pallas_call x1, Pallas kernels, partial_attention(): pl.pallas_call(attention_kernel, out_shape=jax.ShapeDtypeStruct((OUTER, H...  11.4 us
    pallas_call x2, Pallas kernels, project(): pl.pallas_call(project_kernel, out_shape=[jax.ShapeDtypeStruct((rows, OUT...  10.2 us
    ppermute x6, waiting for transfers between devices, xor_to(): return lax.ppermute(x, axis, [(n, n ^ mask) for n in range(size)])  7.91 us
  transfers between devices with their start and end apart: 10, of which 7 were waited for; matrix products, arithmetic and copies ran while one was open for 2% of the time, Pallas kernels for 11%

profile of v2, /device:TPU:97, one launch (start us, length us, event | category | flops | bytes accessed | tf_op | source)
XLA Modules:
  0.0 200.6 jit_solution(2562622703875114201)
XLA Ops:
  0.0 2.4 %broadcast_in_dim.39 = bf16[16,128,512]{2,1,0:T(8,128)(2,1)} broadcast(bf16[128,512]{1,0:T(8,128)(2,1)} %param.5), dimensions={1,2} | broadcast | bytes 2228224 | tf_op jit(solution)/shard_map/broadcast_in_dim | solution.py:262
  2.5 6.9 %all-to-all-start = ((bf16[16,128,512]{2,1,0:T(8,128)(2,1)}), bf16[16,128,512]{2,1,0:T(8,128)(2,1)S(1)}, u32[]{:S(2)}, u32[]{:S(2)}) async-start(bf16[16,128,512]{2,1,0:T(8,128)(2,1)} %broadcast_in_dim.39), calls=%async_computation | async-start | bytes 4194304 | tf_op jit(solution)/shard_map/all_to_all | solution.py:263
  9.4 8.8 %collective-permute-start = (bf16[256,128]{1,0:T(8,128)(2,1)S(1)}, bf16[256,128]{1,0:T(8,128)(2,1)S(1)}, u32[]{:S(2)}, u32[]{:S(2)}) collective-permute-start(bf16[256,128]{1,0:T(8,128)(2,1)S(1)} %pad_maximum_fusion.1), channel_id=1, source_target_pairs={{0,32},{8,40},{16,48},{24,56},{32,0},{40,8},{48,16},{56,24},{1,33}... | collective-permute-start | bytes 196616 | tf_op jit(solution)/shard_map/ppermute | solution.py:237
  18.2 0.1 reshape.27
  18.5 0.4 dynamic-slice_reduce_fusion
  18.9 0.2 select_reduce_fusion
  19.5 3.3 %collective-permute-done = bf16[256,128]{1,0:T(8,128)(2,1)S(1)} collective-permute-done((bf16[256,128]{1,0:T(8,128)(2,1)S(1)}, bf16[256,128]{1,0:T(8,128)(2,1)S(1)}, u32[]{:S(2)}, u32[]{:S(2)}) %collective-permute-start) | collective-permute-done | bytes 65568 | tf_op jit(solution)/shard_map/ppermute | solution.py:237
  22.7 0.7 broadcast_in_dim.38.refs_4_
  23.5 1.9 collective-permute-start.3
  25.4 1.9 collective-permute-start.2
  27.3 5.4 %collective-permute-start.1 = (bf16[512,128]{1,0:T(8,128)(2,1)S(1)}, bf16[512,128]{1,0:T(8,128)(2,1)S(1)}, u32[]{:S(2)}, u32[]{:S(2)}) collective-permute-start(bf16[512,128]{1,0:T(8,128)(2,1)S(1)} %pad_maximum_fusion.refs_0_), channel_id=1, source_target_pairs={{0,8},{8,0},{16,24},{24,16},{32,40},{40,32},{48,56},{56,48},{1,9},... | collective-permute-start | bytes 393224 | tf_op jit(solution)/shard_map/ppermute | solution.py:237
  32.8 2.9 %collective-permute-done.2.refs_2_ = bf16[512,128]{1,0:T(8,128)(2,1)S(1)} collective-permute-done((bf16[512,128]{1,0:T(8,128)(2,1)S(1)}, bf16[512,128]{1,0:T(8,128)(2,1)S(1)}, u32[]{:S(2)}, u32[]{:S(2)}) %collective-permute-start.2) | collective-permute-done | bytes 131104 | tf_op jit(solution)/shard_map/ppermute | solution.py:237
  35.6 1.2 collective-permute-done.1.refs_1_
  36.9 0.6 all-to-all-done.q_ref
  37.5 5.2 %collective-permute-start.5 = (bf16[512,8192]{1,0:T(8,128)(2,1)}, bf16[512,8192]{1,0:T(8,128)(2,1)}, u32[]{:S(2)}, u32[]{:S(2)}) collective-permute-start(bf16[512,8192]{1,0:T(8,128)(2,1)} %w_ref.3), channel_id=1, source_target_pairs={{0,1},{1,0},{2,3},{3,2},{4,5},{5,4},{6,7},{7,6},{8,9},{9,8},{10,11... | collective-permute-start | bytes 25165832 | tf_op jit(solution)/shard_map/ppermute | solution.py:237
  42.8 0.6 reshape.29.sel_ref
  43.4 11.4 %partial_attention.1 = bf16[16,144,512]{2,1,0:T(8,128)(2,1)} custom-call(s32[1]{0:T(128)} %bitcast.2.own_ref, s32[128]{0:T(128)} %reshape.29.sel_ref, bf16[16,128,512]{2,1,0:T(8,128)(2,1)} %copy-done, bf16[512,128]{1,0:T(8,128)(2,1)} %copy-done.2, bf16[512,128]{1,0:T(8,128)(2,1)} %copy-done.9, bf16[512,128]{1,0:T(8,128)(2,1)} %copy-done.8, ...), custom_call_target="tpu_custom_call" | custom-call | flops 8000000000 | bytes 6000000 | tf_op jit(solution)/shard_map/partial_attention/pallas_call | solution.py:129
  54.7 37.2 %all_to_all.10.part_ref = bf16[16,144,512]{2,1,0:T(8,128)(2,1)} all-to-all(bf16[16,144,512]{2,1,0:T(8,128)(2,1)} %partial_attention.1), channel_id=1, replica_groups=mesh['outer'=16,'inner'=8,'tensor'=8] {'outer'}, dimensions={0} | all-to-all | bytes 4718592 | tf_op jit(solution)/shard_map/all_to_all | solution.py:272
  91.9 2.9 %combine.1.x_ref = bf16[128,512]{1,0:T(8,128)(2,1)} custom-call(bf16[16,144,512]{2,1,0:T(8,128)(2,1)} %all_to_all.10.part_ref), custom_call_target="tpu_custom_call" | custom-call | flops 100000000 | bytes 1200000 | tf_op jit(solution)/shard_map/combine/pallas_call | solution.py:177
  94.8 3.5 %collective-permute-start.4 = (bf16[128,512]{1,0:T(8,128)(2,1)}, bf16[128,512]{1,0:T(8,128)(2,1)S(1)}, u32[]{:S(2)}, u32[]{:S(2)}) collective-permute-start(bf16[128,512]{1,0:T(8,128)(2,1)} %combine.1.x_ref), channel_id=1, source_target_pairs={{0,1},{1,0},{2,3},{3,2},{4,5},{5,4},{6,7},{7,6},{8,9},{9,8},{10,11... | collective-permute-start | bytes 393224 | tf_op jit(solution)/shard_map/ppermute | solution.py:237
  98.3 0.6 slice.10.place_ref
  98.9 0.6 collective-permute-done.4.y_ref
  99.5 0.7 copy-done.1
  100.2 3.3 %project.3 = bf16[128,1024]{1,0:T(8,128)(2,1)} custom-call(s32[1]{0:T(128)} %bitcast.7, bf16[128,512]{1,0:T(8,128)(2,1)} %combine.1.x_ref, bf16[128,512]{1,0:T(8,128)(2,1)} %copy-done.1, bf16[512,8192]{1,0:T(8,128)(2,1)} %w_ref.3, bf16[512,8192]{1,0:T(8,128)(2,1)} %collective-permute-done.5.v_ref), custom_call_target="tpu_custom_call" | custom-call | flops 2684354560 | bytes 2097152 | tf_op jit(solution)/shard_map/project/pallas_call | solution.py:208
  103.4 18.8 %collective-permute-start.7 = (bf16[128,1024]{1,0:T(8,128)(2,1)}, bf16[128,1024]{1,0:T(8,128)(2,1)S(1)}, u32[]{:S(2)}, u32[]{:S(2)}) collective-permute-start(bf16[128,1024]{1,0:T(8,128)(2,1)} %project.3), channel_id=1, source_target_pairs={{0,2},{1,7},{2,4},{3,1},{4,6},{5,3},{6,0},{7,5},{8,10},{9,15},{10,... | collective-permute-start | bytes 786440 | tf_op jit(solution)/shard_map/ppermute | solution.py:281
  122.3 7.0 %project.2 = (bf16[128,1024]{1,0:T(8,128)(2,1)}, bf16[128,1024]{1,0:T(8,128)(2,1)}, bf16[128,1024]{1,0:T(8,128)(2,1)}) custom-call(s32[3]{0:T(128)} %slice.10.place_ref, bf16[128,512]{1,0:T(8,128)(2,1)} %combine.1.x_ref, bf16[128,512]{1,0:T(8,128)(2,1)} %copy-done.1, bf16[512,8192]{1,0:T(8,128)(2,1)} %w_ref.3, bf16[512,8192]{1,0:T(8,128)(2,1)} %collective-permute-done.5.v_ref), custom_call_target="tpu_custom_call" | custom-call | flops 8053063680 | bytes 6291456 | tf_op jit(solution)/shard_map/project/pallas_call | solution.py:208
  129.2 1.9 collective-permute-start.6
  131.1 50.6 %collective-permute-done.7 = bf16[128,1024]{1,0:T(8,128)(2,1)S(1)} collective-permute-done((bf16[128,1024]{1,0:T(8,128)(2,1)}, bf16[128,1024]{1,0:T(8,128)(2,1)S(1)}, u32[]{:S(2)}, u32[]{:S(2)}) %collective-permute-start.7) | collective-permute-done | bytes 262176 | tf_op jit(solution)/shard_map/ppermute | solution.py:281
  181.7 1.0 add_convert_fusion.1
  182.7 12.7 %collective-permute-start.8 = (bf16[128,1024]{1,0:T(8,128)(2,1)S(1)}, bf16[128,1024]{1,0:T(8,128)(2,1)S(1)}, u32[]{:S(2)}, u32[]{:S(2)}) collective-permute-start(bf16[128,1024]{1,0:T(8,128)(2,1)S(1)} %add_convert_fusion.1), channel_id=1, source_target_pairs={{0,2},{1,7},{2,4},{3,1},{4,6},{5,3},{6,0},{7,5},{8,10},{9,15},{10,... | collective-permute-start | bytes 786440 | tf_op jit(solution)/shard_map/ppermute | solution.py:284
  195.5 3.3 %collective-permute-done.8 = bf16[128,1024]{1,0:T(8,128)(2,1)S(1)} collective-permute-done((bf16[128,1024]{1,0:T(8,128)(2,1)S(1)}, bf16[128,1024]{1,0:T(8,128)(2,1)S(1)}, u32[]{:S(2)}, u32[]{:S(2)}) %collective-permute-start.8) | collective-permute-done | bytes 262176 | tf_op jit(solution)/shard_map/ppermute | solution.py:284
  198.8 1.8 add_convert_fusion
  (30 shorter events, 0.5 us)
Async XLA Ops:
  2.4 6.9 %copy-start.3 = (bf16[128,128]{1,0:T(8,128)(2,1)S(1)}, bf16[128,128]{1,0:T(8,128)(2,1)}, u32[]{:S(2)}) copy-start(bf16[128,128]{1,0:T(8,128)(2,1)} %param.7) | copy-start | bytes 98308
  2.4 6.9 %copy-start.4 = (bf16[128,128]{1,0:T(8,128)(2,1)S(1)}, bf16[128,128]{1,0:T(8,128)(2,1)}, u32[]{:S(2)}) copy-start(bf16[128,128]{1,0:T(8,128)(2,1)} %param.6) | copy-start | bytes 98308
  2.5 15.8 %copy-start.6 = (s32[256]{0:T(256)S(1)}, s32[256]{0:T(256)}, u32[]{:S(2)}) copy-start(s32[256]{0:T(256)} %param.8) | copy-start | bytes 3076
  2.5 35.1 %all-to-all-start = ((bf16[16,128,512]{2,1,0:T(8,128)(2,1)}), bf16[16,128,512]{2,1,0:T(8,128)(2,1)S(1)}, u32[]{:S(2)}, u32[]{:S(2)}) async-start(bf16[16,128,512]{2,1,0:T(8,128)(2,1)} %broadcast_in_dim.39), calls=%async_computation | async-start | bytes 4194304 | tf_op jit(solution)/shard_map/all_to_all | solution.py:263
  9.4 13.3 %collective-permute-start = (bf16[256,128]{1,0:T(8,128)(2,1)S(1)}, bf16[256,128]{1,0:T(8,128)(2,1)S(1)}, u32[]{:S(2)}, u32[]{:S(2)}) collective-permute-start(bf16[256,128]{1,0:T(8,128)(2,1)S(1)} %pad_maximum_fusion.1), channel_id=1, source_target_pairs={{0,32},{8,40},{16,48},{24,56},{32,0},{40,8},{48,16},{56,24},{1,33}... | collective-permute-start | bytes 196616 | tf_op jit(solution)/shard_map/ppermute | solution.py:237
  19.5 78.9 %copy-start.5 = (s32[4]{0:T(128)}, s32[4]{0:T(128)S(1)}, u32[]{:S(2)}) copy-start(s32[4]{0:T(128)S(1)} %fusion.3) | copy-start | bytes 52
  22.7 20.6 %copy-start.2 = (bf16[512,128]{1,0:T(8,128)(2,1)}, bf16[512,128]{1,0:T(8,128)(2,1)S(1)}, u32[]{:S(2)}) copy-start(bf16[512,128]{1,0:T(8,128)(2,1)S(1)} %pad_maximum_fusion.refs_0_) | copy-start | bytes 393220
  23.5 9.3 %collective-permute-start.3 = (bf16[512,128]{1,0:T(8,128)(2,1)S(1)}, bf16[512,128]{1,0:T(8,128)(2,1)S(1)}, u32[]{:S(2)}, u32[]{:S(2)}) collective-permute-start(bf16[512,128]{1,0:T(8,128)(2,1)S(1)} %pad_maximum_fusion.refs_0_), channel_id=1, source_target_pairs={{0,24},{8,16},{16,8},{24,0},{32,56},{40,48},{48,40},{56,32},{1,25}... | collective-permute-start | bytes 393224 | tf_op jit(solution)/shard_map/ppermute | solution.py:237
  25.4 10.3 %collective-permute-start.2 = (bf16[512,128]{1,0:T(8,128)(2,1)S(1)}, bf16[512,128]{1,0:T(8,128)(2,1)S(1)}, u32[]{:S(2)}, u32[]{:S(2)}) collective-permute-start(bf16[512,128]{1,0:T(8,128)(2,1)S(1)} %pad_maximum_fusion.refs_0_), channel_id=1, source_target_pairs={{0,16},{8,24},{16,0},{24,8},{32,48},{40,56},{48,32},{56,40},{1,17}... | collective-permute-start | bytes 393224 | tf_op jit(solution)/shard_map/ppermute | solution.py:237
  27.3 9.6 %collective-permute-start.1 = (bf16[512,128]{1,0:T(8,128)(2,1)S(1)}, bf16[512,128]{1,0:T(8,128)(2,1)S(1)}, u32[]{:S(2)}, u32[]{:S(2)}) collective-permute-start(bf16[512,128]{1,0:T(8,128)(2,1)S(1)} %pad_maximum_fusion.refs_0_), channel_id=1, source_target_pairs={{0,8},{8,0},{16,24},{24,16},{32,40},{40,32},{48,56},{56,48},{1,9},... | collective-permute-start | bytes 393224 | tf_op jit(solution)/shard_map/ppermute | solution.py:237
  32.8 10.6 %copy-start.7 = (bf16[512,128]{1,0:T(8,128)(2,1)}, bf16[512,128]{1,0:T(8,128)(2,1)S(1)}, u32[]{:S(2)}) copy-start(bf16[512,128]{1,0:T(8,128)(2,1)S(1)} %collective-permute-done.3.refs_3_) | copy-start | bytes 393220
  35.6 7.7 %copy-start.8 = (bf16[512,128]{1,0:T(8,128)(2,1)}, bf16[512,128]{1,0:T(8,128)(2,1)S(1)}, u32[]{:S(2)}) copy-start(bf16[512,128]{1,0:T(8,128)(2,1)S(1)} %collective-permute-done.2.refs_2_) | copy-start | bytes 393220
  36.9 6.5 %copy-start.9 = (bf16[512,128]{1,0:T(8,128)(2,1)}, bf16[512,128]{1,0:T(8,128)(2,1)S(1)}, u32[]{:S(2)}) copy-start(bf16[512,128]{1,0:T(8,128)(2,1)S(1)} %collective-permute-done.1.refs_1_) | copy-start | bytes 393220
  37.5 5.8 %copy-start = (bf16[16,128,512]{2,1,0:T(8,128)(2,1)}, bf16[16,128,512]{2,1,0:T(8,128)(2,1)S(1)}, u32[]{:S(2)}) copy-start(bf16[16,128,512]{2,1,0:T(8,128)(2,1)S(1)} %all-to-all-done.q_ref) | copy-start | bytes 6291460
  37.5 62.0 %collective-permute-start.5 = (bf16[512,8192]{1,0:T(8,128)(2,1)}, bf16[512,8192]{1,0:T(8,128)(2,1)}, u32[]{:S(2)}, u32[]{:S(2)}) collective-permute-start(bf16[512,8192]{1,0:T(8,128)(2,1)} %w_ref.3), channel_id=1, source_target_pairs={{0,1},{1,0},{2,3},{3,2},{4,5},{5,4},{6,7},{7,6},{8,9},{9,8},{10,11... | collective-permute-start | bytes 25165832 | tf_op jit(solution)/shard_map/ppermute | solution.py:237
  94.8 4.7 %collective-permute-start.4 = (bf16[128,512]{1,0:T(8,128)(2,1)}, bf16[128,512]{1,0:T(8,128)(2,1)S(1)}, u32[]{:S(2)}, u32[]{:S(2)}) collective-permute-start(bf16[128,512]{1,0:T(8,128)(2,1)} %combine.1.x_ref), channel_id=1, source_target_pairs={{0,1},{1,0},{2,3},{3,2},{4,5},{5,4},{6,7},{7,6},{8,9},{9,8},{10,11... | collective-permute-start | bytes 393224 | tf_op jit(solution)/shard_map/ppermute | solution.py:237
  99.5 0.7 copy-start.1
  103.4 78.3 %collective-permute-start.7 = (bf16[128,1024]{1,0:T(8,128)(2,1)}, bf16[128,1024]{1,0:T(8,128)(2,1)S(1)}, u32[]{:S(2)}, u32[]{:S(2)}) collective-permute-start(bf16[128,1024]{1,0:T(8,128)(2,1)} %project.3), channel_id=1, source_target_pairs={{0,2},{1,7},{2,4},{3,1},{4,6},{5,3},{6,0},{7,5},{8,10},{9,15},{10,... | collective-permute-start | bytes 786440 | tf_op jit(solution)/shard_map/ppermute | solution.py:281
  129.2 66.3 %collective-permute-start.6 = (bf16[128,1024]{1,0:T(8,128)(2,1)}, bf16[128,1024]{1,0:T(8,128)(2,1)S(1)}, u32[]{:S(2)}, u32[]{:S(2)}) collective-permute-start(bf16[128,1024]{1,0:T(8,128)(2,1)} %get-tuple-element.29), channel_id=1, source_target_pairs={{2,0},{7,1},{4,2},{1,3},{6,4},{3,5},{0,6},{5,7},{10,8},{15,9},{12,... | collective-permute-start | bytes 786440 | tf_op jit(solution)/shard_map/ppermute | solution.py:283
  182.7 16.1 %collective-permute-start.8 = (bf16[128,1024]{1,0:T(8,128)(2,1)S(1)}, bf16[128,1024]{1,0:T(8,128)(2,1)S(1)}, u32[]{:S(2)}, u32[]{:S(2)}) collective-permute-start(bf16[128,1024]{1,0:T(8,128)(2,1)S(1)} %add_convert_fusion.1), channel_id=1, source_target_pairs={{0,2},{1,7},{2,4},{3,1},{4,6},{5,3},{6,0},{7,5},{8,10},{9,15},{10,... | collective-permute-start | bytes 786440 | tf_op jit(solution)/shard_map/ppermute | solution.py:284

commit v3 on v2

--- a/solution.py
+++ b/solution.py
@@ -9,14 +9,14 @@
 
 
 HD = 128
+HEADS = 4
 CH = 64
 ROWS = 2 * CH
 OUTER = 16
 INNER = 8
 FAR = 4
 ZHI = 4
-GROUP = 4
-QC = GROUP * CH
+QC = HEADS * CH
 EXTRA = 16
 NEG = -1e30
 COEF = math.log2(math.e) / math.sqrt(HD)
@@ -38,7 +38,7 @@
 
 def attention_kernel(own_ref, sel_ref, q_ref, *refs):
     pairs = refs[:FAR]
-    late_ref, out_ref, pick, dense, vt_dense, vt_e, vt_l = refs[FAR:]
+    late_ref, oe_ref, ol_ref, pick, dense, vt_dense, vt_e, vt_l = refs[FAR:]
 
     def rows_of(s, at):
         first = (s // FAR) * 2 * ROWS + at
@@ -75,7 +75,7 @@
         own = a == own_ref[0]
         q = q_ref[p]
         stacked = [
-            jnp.concatenate([q[r : r + CH, h * HD : (h + 1) * HD] for h in range(GROUP)], axis=0)
+            jnp.concatenate([q[r : r + CH, h * HD : (h + 1) * HD] for h in range(HEADS)], axis=0)
             for r in (0, CH)
         ]
         q_cat = jnp.concatenate(stacked, axis=1)
@@ -118,26 +118,26 @@
         inv_e = jnp.where(some, 1.0 / jnp.where(some, l_e, 1.0), 0.0)
         lse_e = jnp.where(some, m_e * COEF + jnp.log2(jnp.where(some, l_e, 1.0)), NEG)
         lse_l = m_l * COEF + jnp.log2(l_l)
-        for at, o_t, inv, lse in ((0, o_e, inv_e, lse_e), (QC, o_l, 1.0 / l_l, lse_l)):
+        for ref, o_t, inv, lse in ((oe_ref, o_e, inv_e, lse_e), (ol_ref, o_l, 1.0 / l_l, lse_l)):
             rows = list(three_terms(lse)) + [jnp.zeros((EXTRA - 3, QC), jnp.float32)]
-            out_ref[p, :HD, at : at + QC] = (o_t * inv).astype(jnp.bfloat16)
-            out_ref[p, HD:, at : at + QC] = jnp.concatenate(rows, axis=0).astype(jnp.bfloat16)
-
-
-def partial_attention(own, sel, q_all, kv, late, group):
+            ref[p, :HD, :] = (o_t * inv).astype(jnp.bfloat16)
+            ref[p, HD:, :] = jnp.concatenate(rows, axis=0).astype(jnp.bfloat16)
+
+
+def partial_attention(own, sel, q_all, kv, late):
     n_keys = INNER * CH
     return pl.pallas_call(
         attention_kernel,
-        out_shape=jax.ShapeDtypeStruct((OUTER, HD + EXTRA, 2 * QC), jnp.bfloat16),
+        out_shape=[jax.ShapeDtypeStruct((OUTER, HD + EXTRA, QC), jnp.bfloat16)] * 2,
         grid=(OUTER // PER,),
         in_specs=[
             pl.BlockSpec(memory_space=pltpu.SMEM),
             pl.BlockSpec(memory_space=pltpu.SMEM),
-            pl.BlockSpec((PER, ROWS, GROUP * HD), lambda i: (i, 0, group)),
+            pl.BlockSpec((PER, ROWS, HEADS * HD), lambda i: (i, 0, 0)),
             *[pl.BlockSpec((4 * ROWS, HD), lambda i: (0, 0)) for _ in range(FAR)],
             pl.BlockSpec((PER, 16, n_keys), lambda i: (i, 0, 0)),
         ],
-        out_specs=pl.BlockSpec((PER, HD + EXTRA, 2 * QC), lambda i: (i, 0, 0)),
+        out_specs=[pl.BlockSpec((PER, HD + EXTRA, QC), lambda i: (i, 0, 0))] * 2,
         scratch_shapes=[
             pltpu.VMEM((INNER, 2, CH, 2 * HD), jnp.bfloat16),
             pltpu.VMEM((n_keys + CH, 2 * HD), jnp.bfloat16),
@@ -160,23 +160,20 @@
     for o in range(1, OUTER):
         top = jnp.maximum(top, lse[o])
     total = jnp.zeros_like(top)
-    acc = jnp.zeros((HD, 2 * QC), jnp.float32)
+    acc = jnp.zeros((HD, QC), jnp.float32)
     for o in range(OUTER):
         w = jnp.exp2(lse[o] - top)
         total = total + w
         acc = acc + w * part_ref[o, :HD, :].astype(jnp.float32)
     mixed = (acc * (1.0 / total)).T
-    halves = []
-    for at in (0, QC):
-        heads = [mixed[at + h * CH : at + (h + 1) * CH] for h in range(GROUP)]
-        halves.append(jnp.concatenate(heads, axis=1))
-    out_ref[...] = jnp.concatenate(halves, axis=0).astype(jnp.bfloat16)
+    heads = [mixed[h * CH : (h + 1) * CH] for h in range(HEADS)]
+    out_ref[...] = jnp.concatenate(heads, axis=1).astype(jnp.bfloat16)
 
 
 def combine(parts):
     return pl.pallas_call(
         combine_kernel,
-        out_shape=jax.ShapeDtypeStruct((ROWS, GROUP * HD), jnp.bfloat16),
+        out_shape=jax.ShapeDtypeStruct((CH, HEADS * HD), jnp.bfloat16),
         in_specs=[pl.BlockSpec(memory_space=pltpu.VMEM)],
         out_specs=pl.BlockSpec(memory_space=pltpu.VMEM),
         cost_estimate=pl.CostEstimate(flops=10**8, bytes_accessed=12 * 10**5, transcendentals=0),
@@ -264,25 +261,30 @@
     kv_own = jnp.concatenate([kv_own, kv_far], axis=0)
     kv_own, late, late_rows, place = lax.optimization_barrier((kv_own, late, late_rows, place))
     kv = [kv_own] + [xor_to("inner", INNER, s, kv_own) for s in range(1, FAR)]
-
-    q_all, kv, w_send = lax.optimization_barrier((q_all, kv, w_out))
+    kv, w_send = lax.optimization_barrier((kv, w_out))
     w_other = xor_to("tensor", 2 * ZHI, 1, w_send)
 
-    part = partial_attention(o.reshape(1), late.reshape(-1), q_all, kv, late_rows, 0)
-    part = lax.all_to_all(part, "outer", 0, 0, tiled=True)
-    x = combine(part)
-    y = xor_to("tensor", 2 * ZHI, 1, x)
+    part_e, part_l = partial_attention(o.reshape(1), late.reshape(-1), q_all, kv, late_rows)
+    part_e = lax.all_to_all(part_e, "outer", 0, 0, tiled=True)
+    part_e, part_l = lax.optimization_barrier((part_e, part_l))
+    part_l = lax.all_to_all(part_l, "outer", 0, 0, tiled=True)
 
     count = 2 * ZHI
     ahead_of = [(n + 2 - 4 * (n % 2)) % count for n in range(count)]
     along = [(n, ahead_of[n]) for n in range(count)]
     against = [(ahead_of[n], n) for n in range(count)]
-    (far,) = project(place[:1], x, y, w_out, w_other, 512)
-    relay = lax.ppermute(far, "tensor", along)
-    behind, front, mine = project(place[1:], x, y, w_out, w_other, 512)
-    plain = lax.ppermute(behind, "tensor", against)
-    merged = lax.ppermute(added(front, relay), "tensor", along)
-    return added(mine, plain, merged)
+    results = []
+    for part in (part_e, part_l):
+        x = combine(part)
+        y = xor_to("tensor", count, 1, x)
+        (far,) = project(place[:1], x, y, w_out, w_other, 512)
+        relay = lax.ppermute(far, "tensor", along)
+        behind, front, mine = project(place[1:], x, y, w_out, w_other, 512)
+        plain = lax.ppermute(behind, "tensor", against)
+        front = added(front, relay)
+        merged = lax.ppermute(front, "tensor", along)
+        results.append((mine, plain, merged))
+    return jnp.concatenate([added(*r) for r in results], axis=0)
 
 
 def solution(mesh):

time: 201 us -> 244 us (1.21)
  the two profiles are of different devices: /device:TPU:97 before, /device:TPU:1 now
where the time goes in v3:
time: 244 us; the launch traced here: 243 us
  starting transfers between devices  104 us (43%)
  waiting for transfers between devices  65.3 us (27%)
  Pallas kernels  35.3 us (14%)
  blocking collectives  23.1 us (9%)
  local copies, waits for them, and re-layouts  9.7 us (4%)
  other arithmetic  4.62 us (2%)
    ppermute x7, starting transfers between devices, xor_to(): return lax.ppermute(x, axis, [(n, n ^ mask) for n in range(size)])  42.3 us
    all_to_all x1, waiting for transfers between devices, shards(): q_all = lax.all_to_all(q_many, 'outer', 0, 0, tiled=True)  28.7 us
    ppermute x2, starting transfers between devices, shards(): relay = lax.ppermute(far, 'tensor', along)  26.2 us
    all_to_all x1, blocking collectives, shards(): part_e = lax.all_to_all(part_e, 'outer', 0, 0, tiled=True)  23.1 us
    ppermute x2, waiting for transfers between devices, shards(): merged = lax.ppermute(front, 'tensor', along)  22.9 us
    ppermute x2, starting transfers between devices, shards(): merged = lax.ppermute(front, 'tensor', along)  20.3 us
    pallas_call x4, Pallas kernels, project(): pl.pallas_call(project_kernel, out_shape=[jax.ShapeDtypeStruct((rows, OUT...  19.6 us
    pallas_call x1, Pallas kernels, partial_attention(): pl.pallas_call(attention_kernel, out_shape=[jax.ShapeDtypeStruct((OUTER,...  11.2 us
  transfers between devices with their start and end apart: 15, of which 6 were waited for; matrix products, arithmetic and copies ran while one was open for 3% of the time, Pallas kernels for 15%

profile of v3, /device:TPU:1, one launch (start us, length us, event | category | flops | bytes accessed | tf_op | source)
XLA Modules:
  0.0 242.7 jit_solution(16465131746869548672)
XLA Ops:
  0.8 9.6 %collective-permute-start = (bf16[256,128]{1,0:T(8,128)(2,1)S(1)}, bf16[256,128]{1,0:T(8,128)(2,1)S(1)}, u32[]{:S(2)}, u32[]{:S(2)}) collective-permute-start(bf16[256,128]{1,0:T(8,128)(2,1)S(1)} %pad_maximum_fusion.2), channel_id=1, source_target_pairs={{0,32},{8,40},{16,48},{24,56},{32,0},{40,8},{48,16},{56,24},{1,33}... | collective-permute-start | bytes 196616 | tf_op jit(solution)/shard_map/ppermute | solution.py:234
  13.9 8.1 %collective-permute-start.3 = (bf16[512,128]{1,0:T(8,128)(2,1)S(1)}, bf16[512,128]{1,0:T(8,128)(2,1)S(1)}, u32[]{:S(2)}, u32[]{:S(2)}) collective-permute-start(bf16[512,128]{1,0:T(8,128)(2,1)S(1)} %pad_maximum_fusion.1.refs_0_), channel_id=1, source_target_pairs={{0,24},{8,16},{16,8},{24,0},{32,56},{40,48},{48,40},{56,32},{1,25}... | collective-permute-start | bytes 393224 | tf_op jit(solution)/shard_map/ppermute | solution.py:234
  22.0 1.9 collective-permute-start.2
  23.9 2.2 collective-permute-start.1
  26.1 3.2 %collective-permute-done.2.refs_2_ = bf16[512,128]{1,0:T(8,128)(2,1)S(1)} collective-permute-done((bf16[512,128]{1,0:T(8,128)(2,1)S(1)}, bf16[512,128]{1,0:T(8,128)(2,1)S(1)}, u32[]{:S(2)}, u32[]{:S(2)}) %collective-permute-start.2) | collective-permute-done | bytes 131104 | tf_op jit(solution)/shard_map/ppermute | solution.py:234
  29.3 1.2 collective-permute-done.1.refs_1_
  30.5 11.1 %collective-permute-start.5 = (bf16[512,8192]{1,0:T(8,128)(2,1)}, bf16[512,8192]{1,0:T(8,128)(2,1)}, u32[]{:S(2)}, u32[]{:S(2)}) collective-permute-start(bf16[512,8192]{1,0:T(8,128)(2,1)} %w_ref.7), channel_id=1, source_target_pairs={{0,1},{1,0},{2,3},{3,2},{4,5},{5,4},{6,7},{7,6},{8,9},{9,8},{10,11... | collective-permute-start | bytes 25165832 | tf_op jit(solution)/shard_map/ppermute | solution.py:234
  41.6 2.5 %broadcast_in_dim.39 = bf16[16,128,512]{2,1,0:T(8,128)(2,1)} broadcast(bf16[128,512]{1,0:T(8,128)(2,1)} %param.5), dimensions={1,2} | broadcast | bytes 2228224 | tf_op jit(solution)/shard_map/broadcast_in_dim | solution.py:259
  44.1 3.7 %all-to-all-start = ((bf16[16,128,512]{2,1,0:T(8,128)(2,1)}), bf16[16,128,512]{2,1,0:T(8,128)(2,1)S(1)}, u32[]{:S(2)}, u32[]{:S(2)}) async-start(bf16[16,128,512]{2,1,0:T(8,128)(2,1)} %broadcast_in_dim.39), calls=%async_computation | async-start | bytes 4194304 | tf_op jit(solution)/shard_map/all_to_all | solution.py:260
  48.5 28.7 %all-to-all-done.q_ref = bf16[16,128,512]{2,1,0:T(8,128)(2,1)S(1)} async-done(((bf16[16,128,512]{2,1,0:T(8,128)(2,1)}), bf16[16,128,512]{2,1,0:T(8,128)(2,1)S(1)}, u32[]{:S(2)}, u32[]{:S(2)}) %all-to-all-start) | async-done | bytes 2097184 | tf_op jit(solution)/shard_map/all_to_all | solution.py:260
  77.3 1.4 copy-done.1
  78.7 11.2 %partial_attention.1 = (bf16[16,144,256]{2,1,0:T(8,128)(2,1)}, bf16[16,144,256]{2,1,0:T(8,128)(2,1)}) custom-call(s32[1]{0:T(128)} %bitcast.2.own_ref, s32[128]{0:T(128)} %reshape.29.sel_ref, bf16[16,128,512]{2,1,0:T(8,128)(2,1)} %copy-done.1, bf16[512,128]{1,0:T(8,128)(2,1)} %copy-done.5, bf16[512,128]{1,0:T(8,128)(2,1)} %copy-done.10, ...), custom_call_target="tpu_custom_call" | custom-call | flops 8000000000 | bytes 6000000 | tf_op jit(solution)/shard_map/partial_attention/pallas_call | solution.py:129
  89.9 23.1 %all_to_all.15.part_ref = bf16[16,144,256]{2,1,0:T(8,128)(2,1)} all-to-all(bf16[16,144,256]{2,1,0:T(8,128)(2,1)} %get-tuple-element.32), channel_id=1, replica_groups=mesh['outer'=16,'inner'=8,'tensor'=8] {'outer'}, dimensions={0} | all-to-all | bytes 2359296 | tf_op jit(solution)/shard_map/all_to_all | solution.py:268
  113.0 3.9 %all-to-all-start.2 = ((bf16[16,144,256]{2,1,0:T(8,128)(2,1)}), bf16[16,144,256]{2,1,0:T(8,128)(2,1)S(1)}, u32[]{:S(2)}, u32[]{:S(2)}) async-start(bf16[16,144,256]{2,1,0:T(8,128)(2,1)} %get-tuple-element.39), calls=%async_computation.2 | async-start | bytes 2359296 | tf_op jit(solution)/shard_map/all_to_all | solution.py:270
  116.9 2.2 combine.2.x_ref
  119.1 4.2 %collective-permute-start.4 = (bf16[64,512]{1,0:T(8,128)(2,1)}, bf16[64,512]{1,0:T(8,128)(2,1)S(1)}, u32[]{:S(2)}, u32[]{:S(2)}) collective-permute-start(bf16[64,512]{1,0:T(8,128)(2,1)} %combine.2.x_ref), channel_id=1, source_target_pairs={{0,1},{1,0},{2,3},{3,2},{4,5},{5,4},{6,7},{7,6},{8,9},{9,8},{10,11... | collective-permute-start | bytes 196616 | tf_op jit(solution)/shard_map/ppermute | solution.py:234
  123.9 9.3 %all-to-all-done.2.part_ref = bf16[16,144,256]{2,1,0:T(8,128)(2,1)S(1)} async-done(((bf16[16,144,256]{2,1,0:T(8,128)(2,1)}), bf16[16,144,256]{2,1,0:T(8,128)(2,1)S(1)}, u32[]{:S(2)}, u32[]{:S(2)}) %all-to-all-start.2) | async-done | bytes 1179680 | tf_op jit(solution)/shard_map/all_to_all | solution.py:270
  133.1 1.1 copy-done
  134.2 2.2 combine.3.x_ref
  136.4 5.3 %collective-permute-start.9 = (bf16[64,512]{1,0:T(8,128)(2,1)}, bf16[64,512]{1,0:T(8,128)(2,1)S(1)}, u32[]{:S(2)}, u32[]{:S(2)}) collective-permute-start(bf16[64,512]{1,0:T(8,128)(2,1)} %combine.3.x_ref), channel_id=1, source_target_pairs={{0,1},{1,0},{2,3},{3,2},{4,5},{5,4},{6,7},{7,6},{8,9},{9,8},{10,11... | collective-permute-start | bytes 196616 | tf_op jit(solution)/shard_map/ppermute | solution.py:234
  142.3 3.2 %project.5 = bf16[64,1024]{1,0:T(8,128)(2,1)} custom-call(s32[1]{0:T(128)} %bitcast.7, bf16[64,512]{1,0:T(8,128)(2,1)} %combine.2.x_ref, bf16[64,512]{1,0:T(8,128)(2,1)} %copy-done.2, bf16[512,8192]{1,0:T(8,128)(2,1)} %w_ref.7, bf16[512,8192]{1,0:T(8,128)(2,1)} %collective-permute-done.5.v_ref), custom_call_target="tpu_custom_call" | custom-call | flops 1342177280 | bytes 2097152 | tf_op jit(solution)/shard_map/project/pallas_call | solution.py:205
  145.5 18.1 %collective-permute-start.7 = (bf16[64,1024]{1,0:T(8,128)(2,1)}, bf16[64,1024]{1,0:T(8,128)(2,1)S(1)}, u32[]{:S(2)}, u32[]{:S(2)}) collective-permute-start(bf16[64,1024]{1,0:T(8,128)(2,1)} %project.5), channel_id=1, source_target_pairs={{0,2},{1,7},{2,4},{3,1},{4,6},{5,3},{6,0},{7,5},{8,10},{9,15},{10,... | collective-permute-start | bytes 393224 | tf_op jit(solution)/shard_map/ppermute | solution.py:281
  164.2 3.2 %project.7 = bf16[64,1024]{1,0:T(8,128)(2,1)} custom-call(s32[1]{0:T(128)} %bitcast.8, bf16[64,512]{1,0:T(8,128)(2,1)} %combine.3.x_ref, bf16[64,512]{1,0:T(8,128)(2,1)} %copy-done.3, bf16[512,8192]{1,0:T(8,128)(2,1)} %w_ref.7, bf16[512,8192]{1,0:T(8,128)(2,1)} %collective-permute-done.5.v_ref), custom_call_target="tpu_custom_call" | custom-call | flops 1342177280 | bytes 2097152 | tf_op jit(solution)/shard_map/project/pallas_call | solution.py:205
  167.4 8.2 %collective-permute-start.11 = (bf16[64,1024]{1,0:T(8,128)(2,1)}, bf16[64,1024]{1,0:T(8,128)(2,1)S(1)}, u32[]{:S(2)}, u32[]{:S(2)}) collective-permute-start(bf16[64,1024]{1,0:T(8,128)(2,1)} %project.7), channel_id=1, source_target_pairs={{0,2},{1,7},{2,4},{3,1},{4,6},{5,3},{6,0},{7,5},{8,10},{9,15},{10,... | collective-permute-start | bytes 393224 | tf_op jit(solution)/shard_map/ppermute | solution.py:281
  175.6 6.6 %project.4 = (bf16[64,1024]{1,0:T(8,128)(2,1)}, bf16[64,1024]{1,0:T(8,128)(2,1)}, bf16[64,1024]{1,0:T(8,128)(2,1)}) custom-call(s32[3]{0:T(128)} %slice.12.place_ref, bf16[64,512]{1,0:T(8,128)(2,1)} %combine.2.x_ref, bf16[64,512]{1,0:T(8,128)(2,1)} %copy-done.2, bf16[512,8192]{1,0:T(8,128)(2,1)} %w_ref.7, bf16[512,8192]{1,0:T(8,128)(2,1)} %collective-permute-done.5.v_ref), custom_call_target="tpu_custom_call" | custom-call | flops 4026531840 | bytes 6291456 | tf_op jit(solution)/shard_map/project/pallas_call | solution.py:205
  182.2 5.9 %collective-permute-start.6 = (bf16[64,1024]{1,0:T(8,128)(2,1)}, bf16[64,1024]{1,0:T(8,128)(2,1)S(1)}, u32[]{:S(2)}, u32[]{:S(2)}) collective-permute-start(bf16[64,1024]{1,0:T(8,128)(2,1)} %get-tuple-element.37), channel_id=1, source_target_pairs={{2,0},{7,1},{4,2},{1,3},{6,4},{3,5},{0,6},{5,7},{10,8},{15,9},{12,... | collective-permute-start | bytes 393224 | tf_op jit(solution)/shard_map/ppermute | solution.py:283
  188.2 6.6 %project.6 = (bf16[64,1024]{1,0:T(8,128)(2,1)}, bf16[64,1024]{1,0:T(8,128)(2,1)}, bf16[64,1024]{1,0:T(8,128)(2,1)}) custom-call(s32[3]{0:T(128)} %slice.12.place_ref, bf16[64,512]{1,0:T(8,128)(2,1)} %combine.3.x_ref, bf16[64,512]{1,0:T(8,128)(2,1)} %copy-done.3, bf16[512,8192]{1,0:T(8,128)(2,1)} %w_ref.7, bf16[512,8192]{1,0:T(8,128)(2,1)} %collective-permute-done.5.v_ref), custom_call_target="tpu_custom_call" | custom-call | flops 4026531840 | bytes 6291456 | tf_op jit(solution)/shard_map/project/pallas_call | solution.py:205
  194.8 1.9 collective-permute-start.10
  196.8 12.1 %collective-permute-start.8 = (bf16[64,1024]{1,0:T(8,128)(2,1)S(1)}, bf16[64,1024]{1,0:T(8,128)(2,1)S(1)}, u32[]{:S(2)}, u32[]{:S(2)}) collective-permute-start(bf16[64,1024]{1,0:T(8,128)(2,1)S(1)} %add_convert_fusion.3), channel_id=1, source_target_pairs={{0,2},{1,7},{2,4},{3,1},{4,6},{5,3},{6,0},{7,5},{8,10},{9,15},{10,... | collective-permute-start | bytes 393224 | tf_op jit(solution)/shard_map/ppermute | solution.py:285
  209.8 8.2 %collective-permute-start.12 = (bf16[64,1024]{1,0:T(8,128)(2,1)S(1)}, bf16[64,1024]{1,0:T(8,128)(2,1)S(1)}, u32[]{:S(2)}, u32[]{:S(2)}) collective-permute-start(bf16[64,1024]{1,0:T(8,128)(2,1)S(1)} %add_convert_fusion.1), channel_id=1, source_target_pairs={{0,2},{1,7},{2,4},{3,1},{4,6},{5,3},{6,0},{7,5},{8,10},{9,15},{10,... | collective-permute-start | bytes 393224 | tf_op jit(solution)/shard_map/ppermute | solution.py:285
  218.0 21.6 %collective-permute-done.8 = bf16[64,1024]{1,0:T(8,128)(2,1)S(1)} collective-permute-done((bf16[64,1024]{1,0:T(8,128)(2,1)S(1)}, bf16[64,1024]{1,0:T(8,128)(2,1)S(1)}, u32[]{:S(2)}, u32[]{:S(2)}) %collective-permute-start.8) | collective-permute-done | bytes 131104 | tf_op jit(solution)/shard_map/ppermute | solution.py:285
  239.7 1.3 collective-permute-done.12
  (48 shorter events, 9.4 us)
Async XLA Ops:
  0.8 11.6 %collective-permute-start = (bf16[256,128]{1,0:T(8,128)(2,1)S(1)}, bf16[256,128]{1,0:T(8,128)(2,1)S(1)}, u32[]{:S(2)}, u32[]{:S(2)}) collective-permute-start(bf16[256,128]{1,0:T(8,128)(2,1)S(1)} %pad_maximum_fusion.2), channel_id=1, source_target_pairs={{0,32},{8,40},{16,48},{24,56},{32,0},{40,8},{48,16},{56,24},{1,33}... | collective-permute-start | bytes 196616 | tf_op jit(solution)/shard_map/ppermute | solution.py:234
  12.3 111.0 %copy-start.7 = (s32[4]{0:T(128)}, s32[4]{0:T(128)S(1)}, u32[]{:S(2)}) copy-start(s32[4]{0:T(128)S(1)} %fusion.3) | copy-start | bytes 52
  13.1 30.9 %copy-start.5 = (bf16[512,128]{1,0:T(8,128)(2,1)}, bf16[512,128]{1,0:T(8,128)(2,1)S(1)}, u32[]{:S(2)}) copy-start(bf16[512,128]{1,0:T(8,128)(2,1)S(1)} %pad_maximum_fusion.1.refs_0_) | copy-start | bytes 393220
  13.9 12.2 %collective-permute-start.3 = (bf16[512,128]{1,0:T(8,128)(2,1)S(1)}, bf16[512,128]{1,0:T(8,128)(2,1)S(1)}, u32[]{:S(2)}, u32[]{:S(2)}) collective-permute-start(bf16[512,128]{1,0:T(8,128)(2,1)S(1)} %pad_maximum_fusion.1.refs_0_), channel_id=1, source_target_pairs={{0,24},{8,16},{16,8},{24,0},{32,56},{40,48},{48,40},{56,32},{1,25}... | collective-permute-start | bytes 393224 | tf_op jit(solution)/shard_map/ppermute | solution.py:234
  22.0 7.4 %collective-permute-start.2 = (bf16[512,128]{1,0:T(8,128)(2,1)S(1)}, bf16[512,128]{1,0:T(8,128)(2,1)S(1)}, u32[]{:S(2)}, u32[]{:S(2)}) collective-permute-start(bf16[512,128]{1,0:T(8,128)(2,1)S(1)} %pad_maximum_fusion.1.refs_0_), channel_id=1, source_target_pairs={{0,16},{8,24},{16,0},{24,8},{32,48},{40,56},{48,32},{56,40},{1,17}... | collective-permute-start | bytes 393224 | tf_op jit(solution)/shard_map/ppermute | solution.py:234
  23.9 6.6 %collective-permute-start.1 = (bf16[512,128]{1,0:T(8,128)(2,1)S(1)}, bf16[512,128]{1,0:T(8,128)(2,1)S(1)}, u32[]{:S(2)}, u32[]{:S(2)}) collective-permute-start(bf16[512,128]{1,0:T(8,128)(2,1)S(1)} %pad_maximum_fusion.1.refs_0_), channel_id=1, source_target_pairs={{0,8},{8,0},{16,24},{24,16},{32,40},{40,32},{48,56},{56,48},{1,9},... | collective-permute-start | bytes 393224 | tf_op jit(solution)/shard_map/ppermute | solution.py:234
  26.1 18.0 %copy-start.8 = (bf16[512,128]{1,0:T(8,128)(2,1)}, bf16[512,128]{1,0:T(8,128)(2,1)S(1)}, u32[]{:S(2)}) copy-start(bf16[512,128]{1,0:T(8,128)(2,1)S(1)} %collective-permute-done.3.refs_3_) | copy-start | bytes 393220
  29.3 14.7 %copy-start.9 = (bf16[512,128]{1,0:T(8,128)(2,1)}, bf16[512,128]{1,0:T(8,128)(2,1)S(1)}, u32[]{:S(2)}) copy-start(bf16[512,128]{1,0:T(8,128)(2,1)S(1)} %collective-permute-done.2.refs_2_) | copy-start | bytes 393220
  30.5 13.6 %copy-start.10 = (bf16[512,128]{1,0:T(8,128)(2,1)}, bf16[512,128]{1,0:T(8,128)(2,1)S(1)}, u32[]{:S(2)}) copy-start(bf16[512,128]{1,0:T(8,128)(2,1)S(1)} %collective-permute-done.1.refs_1_) | copy-start | bytes 393220
  30.5 111.2 %collective-permute-start.5 = (bf16[512,8192]{1,0:T(8,128)(2,1)}, bf16[512,8192]{1,0:T(8,128)(2,1)}, u32[]{:S(2)}, u32[]{:S(2)}) collective-permute-start(bf16[512,8192]{1,0:T(8,128)(2,1)} %w_ref.7), channel_id=1, source_target_pairs={{0,1},{1,0},{2,3},{3,2},{4,5},{5,4},{6,7},{7,6},{8,9},{9,8},{10,11... | collective-permute-start | bytes 25165832 | tf_op jit(solution)/shard_map/ppermute | solution.py:234
  44.1 33.2 %all-to-all-start = ((bf16[16,128,512]{2,1,0:T(8,128)(2,1)}), bf16[16,128,512]{2,1,0:T(8,128)(2,1)S(1)}, u32[]{:S(2)}, u32[]{:S(2)}) async-start(bf16[16,128,512]{2,1,0:T(8,128)(2,1)} %broadcast_in_dim.39), calls=%async_computation | async-start | bytes 4194304 | tf_op jit(solution)/shard_map/all_to_all | solution.py:260
  77.3 1.4 copy-start.1
  113.0 20.2 %all-to-all-start.2 = ((bf16[16,144,256]{2,1,0:T(8,128)(2,1)}), bf16[16,144,256]{2,1,0:T(8,128)(2,1)S(1)}, u32[]{:S(2)}, u32[]{:S(2)}) async-start(bf16[16,144,256]{2,1,0:T(8,128)(2,1)} %get-tuple-element.39), calls=%async_computation.2 | async-start | bytes 2359296 | tf_op jit(solution)/shard_map/all_to_all | solution.py:270
  119.1 22.6 %collective-permute-start.4 = (bf16[64,512]{1,0:T(8,128)(2,1)}, bf16[64,512]{1,0:T(8,128)(2,1)S(1)}, u32[]{:S(2)}, u32[]{:S(2)}) collective-permute-start(bf16[64,512]{1,0:T(8,128)(2,1)} %combine.2.x_ref), channel_id=1, source_target_pairs={{0,1},{1,0},{2,3},{3,2},{4,5},{5,4},{6,7},{7,6},{8,9},{9,8},{10,11... | collective-permute-start | bytes 196616 | tf_op jit(solution)/shard_map/ppermute | solution.py:234
  133.1 1.1 copy-start
  136.4 27.1 %collective-permute-start.9 = (bf16[64,512]{1,0:T(8,128)(2,1)}, bf16[64,512]{1,0:T(8,128)(2,1)S(1)}, u32[]{:S(2)}, u32[]{:S(2)}) collective-permute-start(bf16[64,512]{1,0:T(8,128)(2,1)} %combine.3.x_ref), channel_id=1, source_target_pairs={{0,1},{1,0},{2,3},{3,2},{4,5},{5,4},{6,7},{7,6},{8,9},{9,8},{10,11... | collective-permute-start | bytes 196616 | tf_op jit(solution)/shard_map/ppermute | solution.py:234
  141.7 0.6 copy-start.2
  145.5 51.2 %collective-permute-start.7 = (bf16[64,1024]{1,0:T(8,128)(2,1)}, bf16[64,1024]{1,0:T(8,128)(2,1)S(1)}, u32[]{:S(2)}, u32[]{:S(2)}) collective-permute-start(bf16[64,1024]{1,0:T(8,128)(2,1)} %project.5), channel_id=1, source_target_pairs={{0,2},{1,7},{2,4},{3,1},{4,6},{5,3},{6,0},{7,5},{8,10},{9,15},{10,... | collective-permute-start | bytes 393224 | tf_op jit(solution)/shard_map/ppermute | solution.py:281
  163.6 0.6 copy-start.3
  167.4 41.5 %collective-permute-start.11 = (bf16[64,1024]{1,0:T(8,128)(2,1)}, bf16[64,1024]{1,0:T(8,128)(2,1)S(1)}, u32[]{:S(2)}, u32[]{:S(2)}) collective-permute-start(bf16[64,1024]{1,0:T(8,128)(2,1)} %project.7), channel_id=1, source_target_pairs={{0,2},{1,7},{2,4},{3,1},{4,6},{5,3},{6,0},{7,5},{8,10},{9,15},{10,... | collective-permute-start | bytes 393224 | tf_op jit(solution)/shard_map/ppermute | solution.py:281
  182.2 14.5 %copy-start.4 = (bf16[64,1024]{1,0:T(8,128)(2,1)S(1)}, bf16[64,1024]{1,0:T(8,128)(2,1)}, u32[]{:S(2)}) copy-start(bf16[64,1024]{1,0:T(8,128)(2,1)} %get-tuple-element.38) | copy-start | bytes 393220
  182.2 57.4 %copy-start.6 = (bf16[64,1024]{1,0:T(8,128)(2,1)S(1)}, bf16[64,1024]{1,0:T(8,128)(2,1)}, u32[]{:S(2)}) copy-start(bf16[64,1024]{1,0:T(8,128)(2,1)} %get-tuple-element.36) | copy-start | bytes 393220
  182.2 35.8 %collective-permute-start.6 = (bf16[64,1024]{1,0:T(8,128)(2,1)}, bf16[64,1024]{1,0:T(8,128)(2,1)S(1)}, u32[]{:S(2)}, u32[]{:S(2)}) collective-permute-start(bf16[64,1024]{1,0:T(8,128)(2,1)} %get-tuple-element.37), channel_id=1, source_target_pairs={{2,0},{7,1},{4,2},{1,3},{6,4},{3,5},{0,6},{5,7},{10,8},{15,9},{12,... | collective-permute-start | bytes 393224 | tf_op jit(solution)/shard_map/ppermute | solution.py:283
  194.8 44.8 %collective-permute-start.10 = (bf16[64,1024]{1,0:T(8,128)(2,1)}, bf16[64,1024]{1,0:T(8,128)(2,1)S(1)}, u32[]{:S(2)}, u32[]{:S(2)}) collective-permute-start(bf16[64,1024]{1,0:T(8,128)(2,1)} %get-tuple-element.41), channel_id=1, source_target_pairs={{2,0},{7,1},{4,2},{1,3},{6,4},{3,5},{0,6},{5,7},{10,8},{15,9},{12,... | collective-permute-start | bytes 393224 | tf_op jit(solution)/shard_map/ppermute | solution.py:283
  196.8 42.8 %collective-permute-start.8 = (bf16[64,1024]{1,0:T(8,128)(2,1)S(1)}, bf16[64,1024]{1,0:T(8,128)(2,1)S(1)}, u32[]{:S(2)}, u32[]{:S(2)}) collective-permute-start(bf16[64,1024]{1,0:T(8,128)(2,1)S(1)} %add_convert_fusion.3), channel_id=1, source_target_pairs={{0,2},{1,7},{2,4},{3,1},{4,6},{5,3},{6,0},{7,5},{8,10},{9,15},{10,... | collective-permute-start | bytes 393224 | tf_op jit(solution)/shard_map/ppermute | solution.py:285
  209.8 31.2 %collective-permute-start.12 = (bf16[64,1024]{1,0:T(8,128)(2,1)S(1)}, bf16[64,1024]{1,0:T(8,128)(2,1)S(1)}, u32[]{:S(2)}, u32[]{:S(2)}) collective-permute-start(bf16[64,1024]{1,0:T(8,128)(2,1)S(1)} %add_convert_fusion.1), channel_id=1, source_target_pairs={{0,2},{1,7},{2,4},{3,1},{4,6},{5,3},{6,0},{7,5},{8,10},{9,15},{10,... | collective-permute-start | bytes 393224 | tf_op jit(solution)/shard_map/ppermute | solution.py:285
